TPU v7x, 32 devices: a whole 2x2x4 slice. The times are simulated.
32 devices in a mesh: grp: 2 (over y), sp: 16 (over z, x, core).
Axes of the slice: x: 2, y: 2, z: 4, core: 2. Of those that a mesh axis runs over, the one named last changes fastest.
Arguments:
- alpha: float32 [20, 16, 4096], P('grp', None, 'sp'), may hold values from -6 to 6
- ensemble: bfloat16 [20, 3, 16, 4096], P('grp', None, None, 'sp'), may hold values from -6 to 6
- static_std: float32 [3, 16, 4096], P(None, 'grp', 'sp'), may hold values from 0.2 to 1
- control: float32 [3, 16, 4096], P(None, 'grp', 'sp'), may hold values from -6 to 6
- loc_spectrum: float32 [1024], replicated, may hold values from 0.00024414062 to 0.001953125
- obs_cell: int32 [32768], P(('grp', 'sp')), may hold values from 0 to 65535, as said below
- obs_step: int32 [32768], P(('grp', 'sp')), may hold values from 0 to 2
- innovation: float32 [32768], P(('grp', 'sp')), may hold values from -6 to 6
- obs_weight: float32 [32768], P(('grp', 'sp')), may hold values from 0.5 to 4
Outputs:
- grad_alpha: float32 [20, 16, 4096], P('grp', None, 'sp')
- grad_control: float32 [3, 16, 4096], P(None, 'grp', 'sp')
Inputs may be any that keep to these rules, and one draw needn't show every extreme that they name: `obs_cell`: an entry is row * 4096 + column. Entries 1024 * b to 1024 * (b + 1) - 1 lie in the tile of 8 rows from row 8 * (b // 16) and 256 columns from column 256 * (b % 16).
All inputs are finite; a program needn't handle non-finite values.
Results may differ from a plain program's by a relative error of at most 0.0075.
Values may be sent and summed in bfloat16 or wider, within the bound.
A program may use at most 128 MiB of HBM per device.

v0:
```python
import functools
import math

import jax
import jax.numpy as jnp
import numpy as np
from jax import lax
from jax.experimental import pallas as pl
from jax.experimental.pallas import tpu as pltpu
from jax.sharding import PartitionSpec as P

COURANT = 0.4


def tables(parts, cols, waves):
    length = parts * cols
    inner_waves = waves // parts
    k1 = np.arange(parts)
    turn = 2 * np.pi * (np.outer(k1, np.arange(parts)) % parts) / parts
    outer = np.concatenate([np.cos(turn), -np.sin(turn)])
    twist = 2 * np.pi * np.outer(k1, np.arange(cols)) / length
    phase = 2 * np.pi * (np.outer(np.arange(cols), np.arange(inner_waves)) % cols) / cols
    c, s = np.cos(phase), np.sin(phase)
    inner = np.block([[c, -s], [s, c]])
    return [np.asarray(t, np.float32) for t in (outer, np.cos(twist), np.sin(twist), inner)]


EDGE = 128
BF16, F32 = jnp.bfloat16, jnp.float32


def dot(a, b, contract=((1,), (0,))):
    return lax.dot_general(a, b, (contract, ((), ())), preferred_element_type=F32)


def split2(x):
    hi = x.astype(BF16)
    return hi, (x - hi.astype(F32)).astype(BF16)


def right_mul(x, hi, lo):
    x_hi, x_lo = split2(x)
    return dot(x_hi, hi) + dot(x_lo, hi) + dot(x_hi, lo)


def left_mul(hi, lo, x):
    x_hi, x_lo = split2(x)
    return dot(hi, x_hi) + dot(hi, x_lo) + dot(lo, x_hi)


def dx(q):
    width = q.shape[1]
    return 0.5 * (pltpu.roll(q, width - 1, 1) - pltpu.roll(q, 1, 1))


def dy(q):
    rows = q.shape[0]
    at = lax.broadcasted_iota(jnp.int32, q.shape, 0)
    above = jnp.where(at < rows - 1, pltpu.roll(q, rows - 1, 0), 0.0)
    below = jnp.where(at > 0, pltpu.roll(q, 1, 0), 0.0)
    return 0.5 * (above - below)


def model_step(state, rotation):
    h, u, w = state
    h = h - COURANT * (dx(u) + dy(w))
    return h, u - COURANT * dx(h) + rotation * w, w - COURANT * dy(h) - rotation * u


def adjoint_step(state, rotation):
    h, u, w = state
    a = h + COURANT * (dx(u) + dy(w))
    return a, u - rotation * w + COURANT * dx(a), w + rotation * u + COURANT * dy(a)


def kernel(
    groups, parts, spread,
    alpha_ref, std_ref, control_ref, weights_ref,
    cell_ref, step_ref, innovation_ref, obs_weight_ref, *refs,
):
    far, near = refs[:11], refs[13:24]
    kernel_body(groups, parts, spread, alpha_ref, std_ref, control_ref, weights_ref, cell_ref, step_ref,
                innovation_ref, obs_weight_ref, far, near, *near, *refs[11:13], *refs[24:])


def kernel_body(
    groups, parts, spread,
    alpha_ref, std_ref, control_ref, weights_ref,
    cell_ref, step_ref, innovation_ref, obs_weight_ref, far, near,
    ensemble_ref, tw_c_ref, tw_s_ref,
    big_hi, big_lo, bigt_hi, bigt_lo, in_hi, in_lo, int_hi, int_lo,
    grad_alpha_ref, grad_control_ref,
    stage, ens, adjoint, snd, rcv, ex_src, ex_full, ex_low, ex_high,
    send_sem, recv_sem, ex_send, ex_recv, load_sem,
):
    group, part = lax.axis_index("grp"), lax.axis_index("sp")
    left, right = lax.rem(part + parts - 1, parts), lax.rem(part + 1, parts)
    members, rows, cols = alpha_ref.shape
    own, padded = rows // parts, stage.shape[1]
    tile_rows = control_ref.shape[1]
    tile = pl.ds(pl.multiple_of(group * tile_rows, tile_rows), tile_rows)
    items = parts * own * padded

    barrier = pltpu.get_barrier_semaphore()
    for i in range(1, parts):
        pl.semaphore_signal(barrier, inc=1, device_id={"sp": lax.rem(part + i, parts)})
    for i in range(1, groups):
        for at in (left, part, right):
            pl.semaphore_signal(barrier, inc=1, device_id={"grp": lax.rem(group + i, groups), "sp": at})

    loads = [pltpu.make_async_copy(a, b, load_sem.at[i]) for i, (a, b) in enumerate(zip(far, near))]
    for load in loads:
        load.start()
    if padded > members:
        stage[:, members:, :] = jnp.zeros((rows, padded - members, cols), F32)
        for v in range(3):
            ens[v, :, members:, :] = jnp.zeros((rows, padded - members, cols), F32)
    for m in range(members):
        stage[:, m, :] = alpha_ref[m]
    snd[0] = stage[...].astype(BF16).reshape(parts, own, padded, cols)
    cell = cell_ref[...]
    row = jnp.zeros_like(cell)
    for r in range(1, rows):
        row = row + jnp.where(cell >= r * cols * parts, 1, 0)
    col = cell - row * (cols * parts) - part * cols
    slot = step_ref[...] * rows + row
    in_col = (lax.broadcasted_iota(jnp.int32, (cols, cell.shape[1]), 0) == col).astype(F32).astype(BF16)
    in_slot = lax.broadcasted_iota(jnp.int32, (3 * rows, cell.shape[1]), 0) == slot
    pl.semaphore_wait(barrier, parts - 1 + 3 * (groups - 1))
    started = []
    waves = jnp.broadcast_to(weights_ref[...][:, None, :], (parts, own * padded, weights_ref.shape[1]))
    waves = waves.reshape(items, weights_ref.shape[1])

    def all_to_all(phase, source):
        copies = []
        for i in range(1, parts):
            to = lax.rem(part + i, parts)
            copies.append(pltpu.make_async_remote_copy(
                src_ref=source.at[to], dst_ref=rcv.at[phase, part],
                send_sem=send_sem.at[phase, i], recv_sem=recv_sem.at[phase, i],
                device_id={"sp": to},
            ))
            copies[-1].start()
        rcv[phase, part] = source[part]
        return copies

    def finish(copies):
        for copy in copies:
            copy.wait_recv()
        started.extend(copies)

    def filtered(phase):
        x = rcv[phase].reshape(items, cols)
        c, s = tw_c_ref[...], tw_s_ref[...]
        y = dot(big_hi[...], x) + dot(big_lo[...], x)
        re, im = y[:items], y[items:]
        z = right_mul(re * c + im * s, in_hi[:cols], in_lo[:cols])
        z = z + right_mul(im * c - re * s, in_hi[cols:], in_lo[cols:])
        v = right_mul(z * waves, int_hi[...], int_lo[...])
        re, im = v[:, :cols], v[:, cols:]
        out = left_mul(bigt_hi[:, :items], bigt_lo[:, :items], re * c - im * s)
        out = out + left_mul(bigt_hi[:, items:], bigt_lo[:, items:], im * c + re * s)
        return out.astype(BF16).reshape(parts, own, padded, cols)

    def exchange(step):
        copies = []
        first, last = pl.ds(0, EDGE), pl.ds(cols - EDGE, EDGE)
        for i in range(groups):
            to = lax.rem(group + i, groups)
            plans = [(1, right, ex_src.at[step, :, :, last], ex_low), (2, left, ex_src.at[step, :, :, first], ex_high)]
            if i > 0:
                plans.append((0, part, ex_src.at[step], ex_full))
            for kind, at, source, target in plans:
                copies.append(pltpu.make_async_remote_copy(
                    src_ref=source, dst_ref=target.at[step, group],
                    send_sem=ex_send.at[step, kind, i], recv_sem=ex_recv.at[step, kind, i],
                    device_id={"grp": to, "sp": at},
                ))
                copies[-1].start()
        ex_full[step, group] = ex_src[step]
        finish(copies)
        wide = []
        for v in range(3):
            pieces = []
            for buffer in (ex_low, ex_full, ex_high):
                total = buffer[step, 0, v]
                for g in range(1, groups):
                    total = total + buffer[step, g, v]
                pieces.append(total)
            wide.append(jnp.concatenate(pieces, axis=1))
        return wide

    copies = all_to_all(0, snd.at[0])
    loads[0].wait()
    for m in range(members):
        for v in range(3):
            ens[v, :, m, :] = ensemble_ref[m, v].astype(F32)
    for load in loads[1:]:
        load.wait()
    finish(copies)
    snd[1] = filtered(0)
    finish(all_to_all(1, snd.at[1]))
    localized = rcv[1].reshape(rows, padded, cols).astype(F32)
    for v in range(3):
        ex_src[0, v] = spread * jnp.sum(ens[v] * localized, axis=1)
        ex_src[0, v, tile, :] = ex_src[0, v, tile, :] + std_ref[v] * control_ref[v]
    state0 = exchange(0)
    row_at = lax.broadcasted_iota(jnp.int32, (rows, cols + 2 * EDGE), 0).astype(F32)
    rotation = 0.1 + 0.2 * (row_at + 0.5) / rows
    state1 = model_step(state0, rotation)
    state2 = model_step(state1, rotation)
    heights = jnp.concatenate([s[0][:, EDGE:-EDGE] for s in (state0, state1, state2)], axis=0)
    high, low = split2(heights)
    picked = dot(high, in_col) + dot(low, in_col)
    observed = jnp.sum(jnp.where(in_slot, picked, 0.0), axis=0, keepdims=True)
    misfit = obs_weight_ref[...] * (observed - innovation_ref[...])
    high, low = split2(jnp.where(in_slot, misfit, 0.0))
    forcing = dot(high, in_col, ((1,), (1,))) + dot(low, in_col, ((1,), (1,)))
    for t in range(3):
        ex_src[1, t] = forcing[t * rows : (t + 1) * rows]
    forcing = exchange(1)
    zero = jnp.zeros_like(rotation)
    h, u, w = adjoint_step((forcing[2], zero, zero), rotation)
    h, u, w = adjoint_step((h + forcing[1], u, w), rotation)
    weighted = jnp.zeros((rows, padded, cols), F32)
    for v, field in enumerate((h + forcing[0], u, w)):
        field = field[:, EDGE:-EDGE]
        adjoint[v] = field
        half = field.astype(BF16).astype(F32)
        weighted = weighted + ens[v] * half[:, None, :]
    snd[2] = weighted.astype(BF16).reshape(parts, own, padded, cols)
    copies = all_to_all(2, snd.at[2])
    for v in range(3):
        grad_control_ref[v] = control_ref[v] + std_ref[v] * adjoint[v, tile, :]
    finish(copies)
    snd[3] = filtered(2)
    finish(all_to_all(3, snd.at[3]))
    stage[...] = rcv[3].reshape(rows, padded, cols).astype(F32)
    for m in range(members):
        grad_alpha_ref[m] = alpha_ref[m] + spread * stage[:, m, :]
    for copy in started:
        copy.wait_send()


def both(table):
    hi = table.astype(BF16)
    return hi, (table - hi.astype(np.float32)).astype(BF16)


def per_device(alpha, ensemble, static_std, control, loc_spectrum, obs_cell, obs_step, innovation, obs_weight):
    members, rows, cols = alpha.shape
    groups, parts = lax.axis_size("grp"), lax.axis_size("sp")
    spread = 1.0 / math.sqrt(members * groups - 1)
    own = rows // parts
    padded = -(-members // 16) * 16

    outer, tw_c, tw_s, inner = tables(parts, cols, loc_spectrum.shape[0])
    items = own * padded
    big = np.kron(outer, np.eye(items, dtype=np.float32))
    waves = loc_spectrum.reshape(inner.shape[1] // 2, parts).T
    waves = jnp.concatenate([waves, waves], axis=1)
    vmem = pl.BlockSpec(memory_space=pltpu.VMEM)
    operands = (
        alpha, static_std, control, waves,
        obs_cell[None], obs_step[None], innovation[None], obs_weight[None],
    )
    loaded = (
        ensemble,
        np.repeat(tw_c, items, axis=0), np.repeat(tw_s, items, axis=0),
        *both(big), *both(big.T), *both(inner), *both(inner.T),
    )
    return pl.pallas_call(
        functools.partial(kernel, groups, parts, spread),
        out_shape=(
            jax.ShapeDtypeStruct(alpha.shape, F32),
            jax.ShapeDtypeStruct(control.shape, F32),
        ),
        in_specs=[vmem] * len(operands) + [pl.BlockSpec(memory_space=pl.ANY)] * len(loaded),
        out_specs=(vmem, vmem),
        scratch_shapes=[
            *[pltpu.VMEM(t.shape, t.dtype) for t in loaded],
            pltpu.VMEM((rows, padded, cols), F32),
            pltpu.VMEM((3, rows, padded, cols), F32),
            pltpu.VMEM((3, rows, cols), F32),
            pltpu.VMEM((4, parts, own, padded, cols), BF16),
            pltpu.VMEM((4, parts, own, padded, cols), BF16),
            pltpu.VMEM((2, 3, rows, cols), F32),
            pltpu.VMEM((2, groups, 3, rows, cols), F32),
            pltpu.VMEM((2, groups, 3, rows, EDGE), F32),
            pltpu.VMEM((2, groups, 3, rows, EDGE), F32),
            pltpu.SemaphoreType.DMA((4, parts)),
            pltpu.SemaphoreType.DMA((4, parts)),
            pltpu.SemaphoreType.DMA((2, 3, groups)),
            pltpu.SemaphoreType.DMA((2, 3, groups)),
            pltpu.SemaphoreType.DMA((len(loaded),)),
        ],
        compiler_params=pltpu.CompilerParams(collective_id=0, has_side_effects=True, vmem_limit_bytes=60 << 20),
    )(*operands, *loaded)


def solution(mesh):
    flat = P(("grp", "sp"))
    tile = P(None, "grp", "sp")
    return jax.shard_map(
        per_device,
        mesh=mesh,
        in_specs=(P("grp", None, "sp"), P("grp", None, None, "sp"), tile, tile, P(), flat, flat, flat, flat),
        out_specs=(P("grp", None, "sp"), tile),
        check_vma=False,
    )
```

profile of v0, /device:TPU:0, one launch (start us, length us, event | category | flops | bytes accessed | tf_op | source)
XLA Modules:
  0.0 46.2 jit_solution(12399391641240822939)
XLA Ops:
  0.6 0.0 copy-start.1
  0.6 0.7 %copy-done.1 = f32[1024]{0:T(1024)S(1)} copy-done((f32[1024]{0:T(1024)S(1)}, f32[1024]{0:T(1024)}, u32[]{:S(2)}) %copy-start.1) | copy-done | bytes 4120
  1.3 0.1 reshape.7
  1.4 0.1 copy.21
  1.5 0.7 %pad_maximum_fusion.weights_ref = f32[16,128]{1,0:T(8,128)} fusion(f32[16,64]{1,0:T(8,128)S(1)} %bitcast.5), kind=kLoop, calls=%fused_computation | loop fusion | flops 2048 | bytes 12288 | tf_op jit(solution)/shard_map/concatenate | solution.py:261
  2.1 41.8 %shard_map.194 = (f32[10,16,256]{2,1,0:T(8,128)}, f32[3,8,256]{2,1,0:T(8,128)}) custom-call(f32[10,16,256]{2,1,0:T(8,128)} %alpha_ref.1, f32[3,8,256]{2,1,0:T(8,128)} %std_ref.1, f32[3,8,256]{2,1,0:T(8,128)} %control_ref.1, f32[16,128]{1,0:T(8,128)} %pad_maximum_fusion.weights_ref, s32[1,1024]{1,0:T(1,128)} %bitcast.6, s32[1,1024]{1,0:T(1,128)} %bitcast.7, ...), custom_call_target="tpu_custom_call" | custom-call | tf_op jit(solution)/shard_map/pallas_call | solution.py:272
  43.9 0.0 copy-start
  43.9 1.6 %copy.24 = f32[10,16,256]{2,1,0:T(8,128)} copy(f32[10,16,256]{2,1,0:T(8,128)} %get-tuple-element.4) | data formatting | bytes 327680
  45.5 0.0 copy-done
  45.6 0.6 %copy.25 = f32[3,8,256]{2,1,0:T(8,128)} copy(f32[3,8,256]{2,1,0:T(8,128)S(1)} %copy-done) | data formatting | bytes 49152
Async XLA Ops:
  0.6 0.7 %copy-start.1 = (f32[1024]{0:T(1024)S(1)}, f32[1024]{0:T(1024)}, u32[]{:S(2)}) copy-start(f32[1024]{0:T(1024)} %param.23) | copy-start | bytes 12292
  43.9 1.6 %copy-start = (f32[3,8,256]{2,1,0:T(8,128)S(1)}, f32[3,8,256]{2,1,0:T(8,128)}, u32[]{:S(2)}) copy-start(f32[3,8,256]{2,1,0:T(8,128)} %get-tuple-element.5) | copy-start | bytes 73732
where the time goes:
time: 46.3 us; the launch traced here: 46.2 us
  Pallas kernels  41.8 us (90%)
  local copies, waits for them, and re-layouts  3.03 us (7%)
  other arithmetic  0.69 us (1%)
  between operations  0.66 us (1%)
    pallas_call x1, Pallas kernels, per_device(): pl.pallas_call(functools.partial(kernel, groups, parts, spread), out_shap...  41.8 us
    unnamed x6, local copies, waits for them, and re-layouts  2.89 us

commit v1 on v0

v1 whole, which is shorter than its diff:
```python
import functools
import math

import jax
import jax.numpy as jnp
import numpy as np
from jax import lax
from jax.experimental import pallas as pl
from jax.experimental.pallas import tpu as pltpu
from jax.sharding import PartitionSpec as P

COURANT = 0.4
LANES = 128
HALO = 8
SLOTS = 16
BF16, F32 = jnp.bfloat16, jnp.float32
ANY = pl.BlockSpec(memory_space=pl.ANY)


def dot(a, b, contract=((1,), (0,))):
    return lax.dot_general(a, b, (contract, ((), ())), preferred_element_type=F32)


def split2(x):
    hi = x.astype(BF16)
    return hi, (x - hi.astype(F32)).astype(BF16)


def both(table):
    table = np.asarray(table, np.float32)
    hi = table.astype(BF16)
    return hi, (table - hi.astype(np.float32)).astype(BF16)


def add(a, b, sign=1.0):
    re = a[0] + b[0] if sign > 0 else a[0] - b[0]
    if b[1] is None:
        return re, a[1]
    if a[1] is None:
        return re, b[1] if sign > 0 else -b[1]
    return re, a[1] + b[1] if sign > 0 else a[1] - b[1]


def conj(a):
    return a[0], None if a[1] is None else -a[1]


def turn(a, eighths, n):
    at = (eighths % n) / n
    if at == 0:
        return a
    re, im = a
    if at == 0.25:
        return (jnp.zeros_like(re) if im is None else -im), re
    if at == 0.75:
        return (jnp.zeros_like(re) if im is None else im), -re
    c, s = math.cos(2 * math.pi * at), math.sin(2 * math.pi * at)
    if im is None:
        return c * re, s * re
    return c * re - s * im, c * im + s * re


def real_dft(xs):
    n = len(xs)
    if n == 1:
        return [(xs[0], None)]
    if n == 2:
        return [(xs[0] + xs[1], None), (xs[0] - xs[1], None)]
    half = n // 2
    even, odd = real_dft(xs[0::2]), real_dft(xs[1::2])
    out = [None] * (half + 1)
    for k in range(half // 2 + 1):
        t = turn(odd[k], -k, n)
        out[k] = add(even[k], t)
        if half - k != k:
            out[half - k] = conj(add(even[k], t, -1.0))
    return out


def real_sum(zs, n):
    if n == 1:
        return [zs[0][0]]
    if n == 2:
        return [zs[0][0] + zs[1][0], zs[0][0] - zs[1][0]]
    half = n // 2
    even, odd = [], []
    for k in range(half // 2 + 1):
        if half - k == k:
            even.append(zs[k])
            odd.append(turn(zs[k], k, n))
        else:
            other = conj(zs[half - k])
            even.append(add(zs[k], other))
            odd.append(turn(add(zs[k], other, -1.0), k, n))
    even, odd = real_sum(even, half), real_sum(odd, half)
    return [(even, odd)[p % 2][p // 2] for p in range(n)]


def dx(q):
    width = q.shape[1]
    return 0.5 * (pltpu.roll(q, width - 1, 1) - pltpu.roll(q, 1, 1))


def dy(q):
    rows = q.shape[0]
    at = lax.broadcasted_iota(jnp.int32, q.shape, 0)
    above = jnp.where(at < rows - 1, pltpu.roll(q, rows - 1, 0), 0.0)
    below = jnp.where(at > 0, pltpu.roll(q, 1, 0), 0.0)
    return 0.5 * (above - below)


def model_step(state, rotation):
    h, u, w = state
    h = h - COURANT * (dx(u) + dy(w))
    return h, u - COURANT * dx(h) + rotation * w, w - COURANT * dy(h) - rotation * u


def adjoint_step(state, rotation):
    h, u, w = state
    a = h + COURANT * (dx(u) + dy(w))
    return a, u - rotation * w + COURANT * dx(a), w + rotation * u + COURANT * dy(a)


def slot_of(v, m, members):
    spare = min(SLOTS - members, members)
    if v < 2:
        return v * SLOTS + m
    return members + m if m < spare else SLOTS + members + m - spare


def kernel(
    groups, parts, spread,
    alpha_any, ens_any, std_any, control_any, spectrum_any, cell_any, step_any, innovation_any, weight_any,
    fwd_hi_any, fwd_lo_any, inv_hi_any, inv_lo_any, tw_c_any, tw_s_any, pick_any,
    corr_ref, grad_control_ref,
    alpha, ens, std, control, spectrum, cell, step, innovation, weight,
    fwd_hi, fwd_lo, inv_hi, inv_lo, tw_c, tw_s, pick,
    stage, ens_stage, adjoint, waves, fields, wide,
    snd_a, rcv_a, snd_e, rcv_e, snd_i, rcv_i, snd_h, rcv_h, snd_o, rcv_o, rcv_f, edge, rcv_edge,
    load_sem, a_send, a_recv, e_send, e_recv, i_send, i_recv, h_send, h_recv, o_send, o_recv, f_send, f_recv,
):
    group, part = lax.axis_index("grp"), lax.axis_index("sp")
    left, right = lax.rem(part + parts - 1, parts), lax.rem(part + 1, parts)
    members, rows, cols = alpha.shape
    tile_rows = control.shape[1]
    tile = pl.ds(pl.multiple_of(group * tile_rows, tile_rows), tile_rows)
    spare = min(SLOTS - members, members)
    shift = members - spare
    halves = cols // LANES
    residues = parts // 2 + 1
    started = []

    barrier = pltpu.get_barrier_semaphore()
    for j in range(groups):
        for i in range(parts):
            if i + j > 0:
                device = {"grp": lax.rem(group + j, groups), "sp": lax.rem(part + i, parts)}
                pl.semaphore_signal(barrier, inc=1, device_id=device)

    pairs = [
        (alpha_any, alpha), (ens_any, ens), (cell_any, cell), (step_any, step), (innovation_any, innovation),
        (weight_any, weight), (std_any, std), (control_any, control), (spectrum_any, spectrum),
        (fwd_hi_any, fwd_hi), (fwd_lo_any, fwd_lo), (inv_hi_any, inv_hi), (inv_lo_any, inv_lo),
        (tw_c_any, tw_c), (tw_s_any, tw_s), (pick_any, pick),
    ]
    loads = [pltpu.make_async_copy(a, b, load_sem.at[i]) for i, (a, b) in enumerate(pairs)]
    for load in loads:
        load.start()

    loads[0].wait()
    for m in range(members):
        stage[:, m, :] = alpha[m]
    for m in range(SLOTS - members):
        stage[:, members + m, :] = alpha[m] if m < spare else jnp.zeros((rows, cols), F32)
    snd_a[...] = stage[...].astype(BF16)
    loads[1].wait()
    used = set()
    for v in range(3):
        for m in range(members):
            at = slot_of(v, m, members)
            used.add(at)
            ens_stage[:, at, :] = ens[m, v].astype(F32)
    for at in range(2 * SLOTS):
        if at not in used:
            ens_stage[:, at, :] = jnp.zeros((rows, cols), F32)
    snd_e[...] = ens_stage[...].astype(BF16)

    for load in loads[2:]:
        load.wait()
    pitch = -(-tile_rows // 8) * 8
    nx = cols * parts
    first = group * tile_rows
    row = jnp.zeros_like(cell)
    cells = cell[...]
    for r in range(1, tile_rows):
        row = row + jnp.where(cells >= (first + r) * nx, 1, 0)
    col = cells - (first + row) * nx - part * cols
    slot = step[...] * pitch + row
    observations = cells.shape[1]
    in_col = (lax.broadcasted_iota(jnp.int32, (cols, observations), 0) == col).astype(F32).astype(BF16)
    in_slot = lax.broadcasted_iota(jnp.int32, (3 * pitch, observations), 0) == slot
    obs_weight = weight[...]
    values = jnp.concatenate([
        jnp.where(in_slot, obs_weight, 0.0), jnp.where(in_slot, obs_weight * innovation[...], 0.0)
    ], axis=0)
    hi, lo = split2(values)
    summed = dot(hi, in_col, ((1,), (1,))) + dot(lo, in_col, ((1,), (1,)))
    for v in range(3):
        fields[v] = std[v] * control[v]
    for f in range(6):
        fields[3 + f] = summed[f * pitch : f * pitch + tile_rows]
    haloed = (0, 1, 2, 4, 5, 7, 8)
    lane = lax.broadcasted_iota(jnp.int32, (tile_rows, LANES), 1)
    packed = jnp.zeros((tile_rows, LANES), F32)
    for e, f in enumerate(haloed):
        ends = jnp.where(lane < LANES // 2, fields[f, :, :LANES], fields[f, :, cols - LANES :])
        window = (lane >= 2 * HALO * e) & (lane < 2 * HALO * (e + 1))
        packed = jnp.where(window, pltpu.roll(ends, (2 * HALO * e + HALO) % LANES, 1), packed)
    edge[...] = packed

    count = spectrum.shape[1]
    inner = count // parts
    wave = lax.broadcasted_iota(jnp.int32, (SLOTS * (-(-residues // SLOTS)), count), 1)
    residue = lax.broadcasted_iota(jnp.int32, wave.shape, 0)
    weights = jnp.broadcast_to(spectrum[...], wave.shape)
    forward = jnp.where((lax.rem(wave, parts) == residue) & (residue < residues), weights, 0.0)
    mirrored = (lax.rem(wave + residue, parts) == 0) & (residue > 0) & (residue < residues - 1)
    backward = jnp.where(mirrored, weights, 0.0)
    k = lax.broadcasted_iota(jnp.int32, (count, 4 * inner), 0)
    j = lax.rem(lax.broadcasted_iota(jnp.int32, (count, 4 * inner), 1), 2 * inner)
    ahead, behind = k - parts * (j - inner), k - parts * (inner - 1 - j)
    ahead = jnp.where((ahead >= 0) & (ahead < parts), 1.0, 0.0).astype(BF16)
    behind = jnp.where((behind >= 0) & (behind < parts), 1.0, 0.0).astype(BF16)
    f_hi, f_lo = split2(forward)
    b_hi, b_lo = split2(backward)
    waves[...] = dot(f_hi, ahead) + dot(f_lo, ahead) + dot(b_hi, behind) + dot(b_lo, behind)

    pl.semaphore_wait(barrier, groups * parts - 1)

    def all_to_all(source, target, send, recv):
        copies = []
        for i in range(1, parts):
            to = lax.rem(part + i, parts)
            copies.append(pltpu.make_async_remote_copy(
                src_ref=source.at[to], dst_ref=target.at[part],
                send_sem=send.at[i], recv_sem=recv.at[i], device_id={"sp": to},
            ))
            copies[-1].start()
        target[part] = source[part]
        started.extend(copies)
        return copies

    def received(copies):
        for copy in copies:
            copy.wait_recv()

    alpha_copies = all_to_all(snd_a, rcv_a, a_send, a_recv)
    ens_copies = all_to_all(snd_e, rcv_e, e_send, e_recv)
    field_copies = []
    for j in range(groups):
        to = lax.rem(group + j, groups)
        plans = [(1, right, edge, rcv_edge.at[0, group]), (2, left, edge, rcv_edge.at[1, group])]
        if j > 0:
            plans.append((0, part, fields, rcv_f.at[group]))
        for kind, at, source, target in plans:
            field_copies.append(pltpu.make_async_remote_copy(
                src_ref=source, dst_ref=target,
                send_sem=f_send.at[kind, j], recv_sem=f_recv.at[kind, j], device_id={"grp": to, "sp": at},
            ))
            field_copies[-1].start()
    started.extend(field_copies)
    rcv_f[group] = fields[...]

    def filtered(xs):
        pieces = [[x[:, h * LANES : (h + 1) * LANES] for x in xs] for h in range(halves)]
        spectra = [real_dft(piece) for piece in pieces]
        res, ims = [], []
        for k1 in range(residues):
            parts_re, parts_im = [], []
            for h in range(halves):
                c = tw_c[k1 : k1 + 1, h * LANES : (h + 1) * LANES]
                s = tw_s[k1 : k1 + 1, h * LANES : (h + 1) * LANES]
                re, im = spectra[h][k1]
                if k1 == 0:
                    parts_re.append(re)
                    parts_im.append(jnp.zeros_like(re))
                elif im is None:
                    parts_re.append(re * c)
                    parts_im.append(-re * s)
                else:
                    parts_re.append(re * c + im * s)
                    parts_im.append(im * c - re * s)
            res.append(jnp.concatenate(parts_re + parts_im, axis=1))
        y_hi, y_lo = split2(jnp.concatenate(res, axis=0))
        z = dot(y_hi, fwd_hi[...]) + dot(y_lo, fwd_hi[...]) + dot(y_hi, fwd_lo[...])
        z = jnp.concatenate(
            [z[k1 * SLOTS : (k1 + 1) * SLOTS] * waves[k1 : k1 + 1, :] for k1 in range(residues)], axis=0
        )
        z_hi, z_lo = split2(z)
        v = dot(z_hi, inv_hi[...]) + dot(z_lo, inv_hi[...]) + dot(z_hi, inv_lo[...])
        outs = []
        for h in range(halves):
            zs = []
            for k1 in range(residues):
                c = tw_c[k1 : k1 + 1, h * LANES : (h + 1) * LANES]
                s = tw_s[k1 : k1 + 1, h * LANES : (h + 1) * LANES]
                at = slice(k1 * SLOTS, (k1 + 1) * SLOTS)
                re = v[at, h * LANES : (h + 1) * LANES]
                im = v[at, cols + h * LANES : cols + (h + 1) * LANES]
                zs.append((re, im) if k1 == 0 else (re * c - im * s, im * c + re * s))
            outs.append(real_sum(zs, parts))
        return [jnp.concatenate([outs[h][p] for h in range(halves)], axis=1) for p in range(parts)]

    received(alpha_copies)
    localized = filtered([rcv_a[p].astype(F32) for p in range(parts)])
    received(ens_copies)
    at_slot = lax.broadcasted_iota(jnp.int32, (SLOTS, cols), 0)
    firsts, seconds = [], []
    for p in range(parts):
        loc = localized[p].astype(BF16).astype(F32)
        moved = jnp.where(at_slot < members, loc, pltpu.roll(loc, shift, 0)) if shift else loc
        firsts.append(rcv_e[p, :SLOTS].astype(F32) * loc)
        seconds.append(rcv_e[p, SLOTS:].astype(F32) * moved)
    a_hi, a_lo = split2(jnp.concatenate(firsts, axis=0))
    b_hi, b_lo = split2(jnp.concatenate(seconds, axis=0))
    pick_a, pick_b = pick[:, : parts * SLOTS], pick[:, parts * SLOTS :]
    inc = spread * (dot(pick_a, a_hi) + dot(pick_a, a_lo) + dot(pick_b, b_hi) + dot(pick_b, b_lo))
    lane = lax.broadcasted_iota(jnp.int32, (parts, LANES), 1)
    packed = jnp.zeros((parts, LANES), F32)
    for v in range(3):
        field = inc[v * parts : (v + 1) * parts]
        for h in range(halves):
            snd_i[:, v * halves + h, :] = field[:, h * LANES : (h + 1) * LANES]
        after = pltpu.roll(field[:, :LANES], parts - 1, 0)
        before = pltpu.roll(field[:, cols - LANES :], 1, 0)
        ends = pltpu.roll(jnp.where(lane < LANES // 2, after, before), 2 * HALO * v + HALO, 1)
        packed = jnp.where((lane >= 2 * HALO * v) & (lane < 2 * HALO * (v + 1)), ends, packed)
    snd_i[:, 3 * halves, :] = packed
    copies = []
    for i in range(parts):
        for j in range(groups):
            if i + j > 0:
                g, to = lax.rem(group + j, groups), lax.rem(part + i, parts)
                copies.append(pltpu.make_async_remote_copy(
                    src_ref=snd_i.at[to], dst_ref=rcv_i.at[group, part],
                    send_sem=i_send.at[i, j], recv_sem=i_recv.at[i, j], device_id={"grp": g, "sp": to},
                ))
                copies[-1].start()
    rcv_i[group, part] = snd_i[part]
    started.extend(copies)

    received(field_copies)
    lane = lax.broadcasted_iota(jnp.int32, (tile_rows, LANES), 1)
    for g in range(groups):
        at = slice(g * tile_rows, (g + 1) * tile_rows)
        for f in range(9):
            wide[f, at, :cols] = rcv_f[g, f]
            if f in haloed:
                back = LANES - (2 * HALO * haloed.index(f) + HALO)
                before, after = (pltpu.roll(rcv_edge[side, g], back, 1) for side in (0, 1))
                wide[f, at, cols:] = jnp.where(lane < LANES // 2, after, before)
            else:
                wide[f, at, cols:] = jnp.zeros((tile_rows, LANES), F32)

    received(copies)

    def gathered(index):
        total = rcv_i[0, :, index, :]
        for g in range(1, groups):
            total = total + rcv_i[g, :, index, :]
        return total

    ends = gathered(3 * halves)
    state0 = []
    for v in range(3):
        pieces = [gathered(v * halves + h) for h in range(halves)]
        pieces.append(pltpu.roll(ends, LANES - (2 * HALO * v + HALO), 1))
        state0.append(jnp.concatenate(pieces, axis=1) + wide[v])
    row_at = lax.broadcasted_iota(jnp.int32, (rows, cols + LANES), 0).astype(F32)
    rotation = 0.1 + 0.2 * (row_at + 0.5) / rows
    state1 = model_step(state0, rotation)
    state2 = model_step(state1, rotation)
    forcing = [wide[3 + t] * s[0] - wide[6 + t] for t, s in enumerate((state0, state1, state2))]
    zero = jnp.zeros_like(rotation)
    h, u, w = adjoint_step((forcing[2], zero, zero), rotation)
    h, u, w = adjoint_step((h + forcing[1], u, w), rotation)
    for v, field in enumerate((h + forcing[0], u, w)):
        field = field[:, :cols]
        adjoint[v] = field
        half = field.astype(BF16).astype(F32)
        for h in range(halves):
            snd_h[:, v * halves + h, :] = half[:, h * LANES : (h + 1) * LANES]
    copies = all_to_all(snd_h, rcv_h, h_send, h_recv)
    for v in range(3):
        grad_control_ref[v] = control[v] + std[v] * adjoint[v, tile, :]
    received(copies)
    weighted = []
    for p in range(parts):
        halfs = []
        for v in range(3):
            pieces = [
                jnp.broadcast_to(rcv_h[p, v * halves + h : v * halves + h + 1, :], (SLOTS, LANES)) for h in range(halves)
            ]
            halfs.append(jnp.concatenate(pieces, axis=1))
        a = rcv_e[p, :SLOTS].astype(F32) * jnp.where(at_slot < members, halfs[0], halfs[2])
        b = rcv_e[p, SLOTS:].astype(F32) * jnp.where(at_slot < members, halfs[1], halfs[2])
        own = jnp.where(at_slot < spare, pltpu.roll(a, SLOTS - members, 0), 0.0)
        if shift:
            own = jnp.where((at_slot >= spare) & (at_slot < members), pltpu.roll(b, SLOTS - shift, 0), own)
        weighted.append(a + b + own)
    outs = filtered(weighted)
    for p in range(parts):
        snd_o[p] = outs[p].astype(BF16)
    received(all_to_all(snd_o, rcv_o, o_send, o_recv))
    stage[...] = rcv_o[...].astype(F32)
    for m in range(members):
        corr_ref[m] = alpha[m] + spread * stage[:, m, :]
    for copy in started:
        copy.wait_send()


def tables(parts, cols, waves, members):
    length = parts * cols
    inner = waves // parts
    residues = parts // 2 + 1
    twist = 2 * np.pi * np.outer(np.arange(residues), np.arange(cols)) / length
    quotient = np.arange(-inner, inner)
    phase = 2 * np.pi * (np.outer(np.arange(cols), quotient) % cols) / cols
    c, s = np.cos(phase), np.sin(phase)
    forward = np.block([[c, -s], [s, c]])
    pick = np.zeros((3 * parts, 2, parts, SLOTS), np.float32)
    for p in range(parts):
        for v in range(3):
            for m in range(members):
                at = slot_of(v, m, members)
                pick[v * parts + p, at // SLOTS, p, at % SLOTS] = 1.0
    return (
        *both(forward), *both(forward.T.copy()), np.cos(twist).astype(np.float32), np.sin(twist).astype(np.float32),
        pick.reshape(3 * parts, 2 * parts * SLOTS).astype(BF16),
    )


def per_device(alpha, ensemble, static_std, control, loc_spectrum, obs_cell, obs_step, innovation, obs_weight):
    members, rows, cols = alpha.shape
    groups, parts = lax.axis_size("grp"), lax.axis_size("sp")
    spread = 1.0 / math.sqrt(members * groups - 1)
    assert rows == parts and 3 * members <= 2 * SLOTS
    tile_rows = control.shape[1]
    residues = parts // 2 + 1
    inner = loc_spectrum.shape[0] // parts
    operands = (
        alpha, ensemble, static_std, control, loc_spectrum[None],
        obs_cell[None], obs_step[None], innovation[None], obs_weight[None],
        *tables(parts, cols, loc_spectrum.shape[0], members),
    )
    message = (8 * (-(-(3 * cols // LANES + 1) // 8)), LANES)
    vmem = pl.BlockSpec(memory_space=pltpu.VMEM)
    dma = pltpu.SemaphoreType.DMA
    corr, grad_control = pl.pallas_call(
        functools.partial(kernel, groups, parts, spread),
        out_shape=(
            jax.ShapeDtypeStruct(alpha.shape, F32),
            jax.ShapeDtypeStruct(control.shape, F32),
        ),
        in_specs=[ANY] * len(operands),
        out_specs=(vmem, vmem),
        scratch_shapes=[
            *[pltpu.VMEM(t.shape, t.dtype) for t in operands],
            pltpu.VMEM((rows, SLOTS, cols), F32),
            pltpu.VMEM((rows, 2 * SLOTS, cols), F32),
            pltpu.VMEM((3, rows, cols), F32),
            pltpu.VMEM((SLOTS * (-(-residues // SLOTS)), 4 * inner), F32),
            pltpu.VMEM((9, tile_rows, cols), F32),
            pltpu.VMEM((9, rows, cols + LANES), F32),
            pltpu.VMEM((parts, SLOTS, cols), BF16), pltpu.VMEM((parts, SLOTS, cols), BF16),
            pltpu.VMEM((parts, 2 * SLOTS, cols), BF16), pltpu.VMEM((parts, 2 * SLOTS, cols), BF16),
            pltpu.VMEM((parts, *message), F32), pltpu.VMEM((groups, parts, *message), F32),
            pltpu.VMEM((parts, *message), F32), pltpu.VMEM((parts, *message), F32),
            pltpu.VMEM((parts, SLOTS, cols), BF16), pltpu.VMEM((parts, SLOTS, cols), BF16),
            pltpu.VMEM((groups, 9, tile_rows, cols), F32),
            pltpu.VMEM((tile_rows, LANES), F32), pltpu.VMEM((2, groups, tile_rows, LANES), F32),
            dma((len(operands),)),
            dma((parts,)), dma((parts,)), dma((parts,)), dma((parts,)),
            dma((parts, groups)), dma((parts, groups)),
            dma((parts,)), dma((parts,)), dma((parts,)), dma((parts,)),
            dma((3, groups)), dma((3, groups)),
        ],
        compiler_params=pltpu.CompilerParams(collective_id=0, has_side_effects=True, vmem_limit_bytes=40 << 20),
    )(*operands)
    return corr, grad_control


def solution(mesh):
    flat = P(("grp", "sp"))
    tile = P(None, "grp", "sp")
    return jax.shard_map(
        per_device,
        mesh=mesh,
        in_specs=(P("grp", None, "sp"), P("grp", None, None, "sp"), tile, tile, P(), flat, flat, flat, flat),
        out_specs=(P("grp", None, "sp"), tile),
        check_vma=False,
    )
```

time: 46.3 us -> 50.2 us (1.084); the launches traced: 46.2 us -> 49.5 us
  local copies, waits for them, and re-layouts: 3.03 us -> 14.1 us
  Pallas kernels: 41.8 us -> 34.7 us
  other arithmetic: 0.69 us -> 0 us
    unnamed x6 -> x34, local copies, waits for them, and re-layouts: 2.89 us -> 14.1 us
    pallas_call x1, Pallas kernels: 41.8 us -> 34.7 us  [per_device(): pl.pallas_call(functools.partial(kernel, groups, parts, spread), out_shap...]
    concatenate x1 -> x0, other arithmetic: 0.69 us -> none  [per_device(): waves = jnp.concatenate([waves, waves], axis=1)]
where the time goes in v1:
time: 50.2 us; the launch traced here: 49.5 us
  Pallas kernels  34.7 us (69%)
  local copies, waits for them, and re-layouts  14.1 us (28%)
  between operations  0.67 us (1%)
    pallas_call x1, Pallas kernels, per_device(): pl.pallas_call(functools.partial(kernel, groups, parts, spread), out_shap...  34.7 us
    unnamed x34, local copies, waits for them, and re-layouts  14.1 us

profile of v1, /device:TPU:0, one launch (start us, length us, event | category | flops | bytes accessed | tf_op | source)
XLA Modules:
  0.0 49.5 jit_solution(13768029821723538289)
XLA Ops:
  0.6 0.0 copy-start.9
  0.6 0.7 %copy-done.9 = f32[9,256]{1,0:T(8,128)S(1)} copy-done((f32[9,256]{1,0:T(8,128)S(1)}, f32[9,256]{1,0:T(8,128)}, u32[]{:S(2)}) %copy-start.9) | copy-done | bytes 9240
  1.4 0.0 copy-start
  1.4 0.9 %copy-done = bf16[256,512]{1,0:T(8,128)(2,1)S(1)} copy-done((bf16[256,512]{1,0:T(8,128)(2,1)S(1)}, bf16[256,512]{1,0:T(8,128)(2,1)}, u32[]{:S(2)}) %copy-start) | copy-done | bytes 262168
  2.3 0.0 copy-start.1
  2.3 0.9 %copy-done.1 = bf16[256,512]{1,0:T(8,128)(2,1)S(1)} copy-done((bf16[256,512]{1,0:T(8,128)(2,1)S(1)}, bf16[256,512]{1,0:T(8,128)(2,1)}, u32[]{:S(2)}) %copy-start.1) | copy-done | bytes 262168
  3.3 0.0 copy-start.2
  3.3 0.9 %copy-done.2 = bf16[512,256]{1,0:T(8,128)(2,1)S(1)} copy-done((bf16[512,256]{1,0:T(8,128)(2,1)S(1)}, bf16[512,256]{1,0:T(8,128)(2,1)}, u32[]{:S(2)}) %copy-start.2) | copy-done | bytes 262168
  4.2 0.0 copy-start.3
  4.2 0.9 %copy-done.3 = bf16[512,256]{1,0:T(8,128)(2,1)S(1)} copy-done((bf16[512,256]{1,0:T(8,128)(2,1)S(1)}, bf16[512,256]{1,0:T(8,128)(2,1)}, u32[]{:S(2)}) %copy-start.3) | copy-done | bytes 262168
  5.2 0.0 copy-start.4
  5.2 0.9 %copy-done.4 = bf16[10,3,16,256]{3,2,1,0:T(8,128)(2,1)S(1)} copy-done((bf16[10,3,16,256]{3,2,1,0:T(8,128)(2,1)S(1)}, bf16[10,3,16,256]{3,2,1,0:T(8,128)(2,1)}, u32[]{:S(2)}) %copy-start.4) | copy-done | bytes 245784
  6.1 0.0 copy-start.5
  6.1 0.9 %copy-done.5 = f32[10,16,256]{2,1,0:T(8,128)S(1)} copy-done((f32[10,16,256]{2,1,0:T(8,128)S(1)}, f32[10,16,256]{2,1,0:T(8,128)}, u32[]{:S(2)}) %copy-start.5) | copy-done | bytes 163864
  7.0 0.0 copy-start.6
  7.0 0.8 %copy-done.6 = bf16[48,512]{1,0:T(8,128)(2,1)S(1)} copy-done((bf16[48,512]{1,0:T(8,128)(2,1)S(1)}, bf16[48,512]{1,0:T(8,128)(2,1)}, u32[]{:S(2)}) %copy-start.6) | copy-done | bytes 49176
  7.8 0.0 copy-start.7
  7.8 0.7 %copy-done.7 = f32[3,8,256]{2,1,0:T(8,128)S(1)} copy-done((f32[3,8,256]{2,1,0:T(8,128)S(1)}, f32[3,8,256]{2,1,0:T(8,128)}, u32[]{:S(2)}) %copy-start.7) | copy-done | bytes 24600
  8.6 0.0 copy-start.8
  8.6 0.7 %copy-done.8 = f32[3,8,256]{2,1,0:T(8,128)S(1)} copy-done((f32[3,8,256]{2,1,0:T(8,128)S(1)}, f32[3,8,256]{2,1,0:T(8,128)}, u32[]{:S(2)}) %copy-start.8) | copy-done | bytes 24600
  9.3 0.0 copy-start.10
  9.3 0.7 %copy-done.10 = f32[9,256]{1,0:T(8,128)S(1)} copy-done((f32[9,256]{1,0:T(8,128)S(1)}, f32[9,256]{1,0:T(8,128)}, u32[]{:S(2)}) %copy-start.10) | copy-done | bytes 9240
  10.0 0.0 copy-start.11
  10.0 0.7 %copy-done.11 = f32[1024]{0:T(1024)S(1)} copy-done((f32[1024]{0:T(1024)S(1)}, f32[1024]{0:T(1024)}, u32[]{:S(2)}) %copy-start.11) | copy-done | bytes 4120
  10.7 0.0 copy-start.12
  10.7 0.7 %copy-done.12 = s32[1024]{0:T(1024)S(1)} copy-done((s32[1024]{0:T(1024)S(1)}, s32[1024]{0:T(1024)}, u32[]{:S(2)}) %copy-start.12) | copy-done | bytes 4120
  11.4 0.0 copy-start.13
  11.4 0.7 %copy-done.13 = s32[1024]{0:T(1024)S(1)} copy-done((s32[1024]{0:T(1024)S(1)}, s32[1024]{0:T(1024)}, u32[]{:S(2)}) %copy-start.13) | copy-done | bytes 4120
  12.1 0.0 copy-start.14
  12.1 0.7 %copy-done.14 = f32[1024]{0:T(1024)S(1)} copy-done((f32[1024]{0:T(1024)S(1)}, f32[1024]{0:T(1024)}, u32[]{:S(2)}) %copy-start.14) | copy-done | bytes 4120
  12.8 0.0 copy-start.15
  12.8 0.7 %copy-done.15 = f32[1024]{0:T(1024)S(1)} copy-done((f32[1024]{0:T(1024)S(1)}, f32[1024]{0:T(1024)}, u32[]{:S(2)}) %copy-start.15) | copy-done | bytes 4120
  13.4 34.7 %shard_map.167 = (f32[10,16,256]{2,1,0:T(8,128)S(1)}, f32[3,8,256]{2,1,0:T(8,128)S(1)}) custom-call(f32[10,16,256]{2,1,0:T(8,128)S(1)} %copy-done.5, bf16[10,3,16,256]{3,2,1,0:T(8,128)(2,1)S(1)} %copy-done.4, f32[3,8,256]{2,1,0:T(8,128)S(1)} %copy-done.7, f32[3,8,256]{2,1,0:T(8,128)S(1)} %copy-done.8, f32[1,1024]{1,0:T(1,128)S(1)} %bitcast.5, ...), custom_call_target="tpu_custom_call" | custom-call | tf_op jit(solution)/shard_map/pallas_call | solution.py:459
  48.2 0.7 %copy.20 = f32[10,16,256]{2,1,0:T(8,128)} copy(f32[10,16,256]{2,1,0:T(8,128)S(1)} %get-tuple-element.4) | data formatting | bytes 327680
  48.9 0.6 %copy.21 = f32[3,8,256]{2,1,0:T(8,128)} copy(f32[3,8,256]{2,1,0:T(8,128)S(1)} %get-tuple-element.5) | data formatting | bytes 49152
Async XLA Ops:
  0.6 0.7 %copy-start.9 = (f32[9,256]{1,0:T(8,128)S(1)}, f32[9,256]{1,0:T(8,128)}, u32[]{:S(2)}) copy-start(f32[9,256]{1,0:T(8,128)} %constant.19.clone.tw_s_any) | copy-start | bytes 27652
  1.4 0.9 %copy-start = (bf16[256,512]{1,0:T(8,128)(2,1)S(1)}, bf16[256,512]{1,0:T(8,128)(2,1)}, u32[]{:S(2)}) copy-start(bf16[256,512]{1,0:T(8,128)(2,1)} %constant.17.clone.inv_lo_any) | copy-start | bytes 786436
  2.3 0.9 %copy-start.1 = (bf16[256,512]{1,0:T(8,128)(2,1)S(1)}, bf16[256,512]{1,0:T(8,128)(2,1)}, u32[]{:S(2)}) copy-start(bf16[256,512]{1,0:T(8,128)(2,1)} %constant.16.clone.inv_hi_any) | copy-start | bytes 786436
  3.3 0.9 %copy-start.2 = (bf16[512,256]{1,0:T(8,128)(2,1)S(1)}, bf16[512,256]{1,0:T(8,128)(2,1)}, u32[]{:S(2)}) copy-start(bf16[512,256]{1,0:T(8,128)(2,1)} %constant.15.clone.fwd_lo_any) | copy-start | bytes 786436
  4.2 0.9 %copy-start.3 = (bf16[512,256]{1,0:T(8,128)(2,1)S(1)}, bf16[512,256]{1,0:T(8,128)(2,1)}, u32[]{:S(2)}) copy-start(bf16[512,256]{1,0:T(8,128)(2,1)} %constant.14.clone.fwd_hi_any) | copy-start | bytes 786436
  5.2 0.9 %copy-start.4 = (bf16[10,3,16,256]{3,2,1,0:T(8,128)(2,1)S(1)}, bf16[10,3,16,256]{3,2,1,0:T(8,128)(2,1)}, u32[]{:S(2)}) copy-start(bf16[10,3,16,256]{3,2,1,0:T(8,128)(2,1)} %ens_any.1) | copy-start | bytes 737284
  6.1 0.9 %copy-start.5 = (f32[10,16,256]{2,1,0:T(8,128)S(1)}, f32[10,16,256]{2,1,0:T(8,128)}, u32[]{:S(2)}) copy-start(f32[10,16,256]{2,1,0:T(8,128)} %alpha_any.1) | copy-start | bytes 491524
  7.0 0.8 %copy-start.6 = (bf16[48,512]{1,0:T(8,128)(2,1)S(1)}, bf16[48,512]{1,0:T(8,128)(2,1)}, u32[]{:S(2)}) copy-start(bf16[48,512]{1,0:T(8,128)(2,1)} %constant.20.clone.pick_any) | copy-start | bytes 147460
  7.8 0.7 %copy-start.7 = (f32[3,8,256]{2,1,0:T(8,128)S(1)}, f32[3,8,256]{2,1,0:T(8,128)}, u32[]{:S(2)}) copy-start(f32[3,8,256]{2,1,0:T(8,128)} %std_any.1) | copy-start | bytes 73732
  8.6 0.7 %copy-start.8 = (f32[3,8,256]{2,1,0:T(8,128)S(1)}, f32[3,8,256]{2,1,0:T(8,128)}, u32[]{:S(2)}) copy-start(f32[3,8,256]{2,1,0:T(8,128)} %control_any.1) | copy-start | bytes 73732
  9.3 0.7 %copy-start.10 = (f32[9,256]{1,0:T(8,128)S(1)}, f32[9,256]{1,0:T(8,128)}, u32[]{:S(2)}) copy-start(f32[9,256]{1,0:T(8,128)} %constant.18.clone.tw_c_any) | copy-start | bytes 27652
  10.0 0.7 %copy-start.11 = (f32[1024]{0:T(1024)S(1)}, f32[1024]{0:T(1024)}, u32[]{:S(2)}) copy-start(f32[1024]{0:T(1024)} %param.20) | copy-start | bytes 12292
  10.7 0.7 %copy-start.12 = (s32[1024]{0:T(1024)S(1)}, s32[1024]{0:T(1024)}, u32[]{:S(2)}) copy-start(s32[1024]{0:T(1024)} %param.21) | copy-start | bytes 12292
  11.4 0.7 %copy-start.13 = (s32[1024]{0:T(1024)S(1)}, s32[1024]{0:T(1024)}, u32[]{:S(2)}) copy-start(s32[1024]{0:T(1024)} %param.22) | copy-start | bytes 12292
  12.1 0.7 %copy-start.14 = (f32[1024]{0:T(1024)S(1)}, f32[1024]{0:T(1024)}, u32[]{:S(2)}) copy-start(f32[1024]{0:T(1024)} %param.23) | copy-start | bytes 12292
  12.8 0.7 %copy-start.15 = (f32[1024]{0:T(1024)S(1)}, f32[1024]{0:T(1024)}, u32[]{:S(2)}) copy-start(f32[1024]{0:T(1024)} %param.24) | copy-start | bytes 12292

commit v2 on v1

--- a/solution.py
+++ b/solution.py
@@ -14,7 +14,7 @@
 HALO = 8
 SLOTS = 16
 BF16, F32 = jnp.bfloat16, jnp.float32
-ANY = pl.BlockSpec(memory_space=pl.ANY)
+HBM = pl.BlockSpec(memory_space=pltpu.HBM)
 
 
 def dot(a, b, contract=((1,), (0,))):
@@ -173,6 +173,26 @@
     for m in range(SLOTS - members):
         stage[:, members + m, :] = alpha[m] if m < spare else jnp.zeros((rows, cols), F32)
     snd_a[...] = stage[...].astype(BF16)
+    def all_to_all(source, target, send, recv):
+        copies = []
+        for i in range(1, parts):
+            to = lax.rem(part + i, parts)
+            copies.append(pltpu.make_async_remote_copy(
+                src_ref=source.at[to], dst_ref=target.at[part],
+                send_sem=send.at[i], recv_sem=recv.at[i], device_id={"sp": to},
+            ))
+            copies[-1].start()
+        target[part] = source[part]
+        started.extend(copies)
+        return copies
+
+    def received(copies):
+        for copy in copies:
+            copy.wait_recv()
+
+    pl.semaphore_wait(barrier, groups * parts - 1)
+
+    alpha_copies = all_to_all(snd_a, rcv_a, a_send, a_recv)
     loads[1].wait()
     used = set()
     for v in range(3):
@@ -185,39 +205,9 @@
             ens_stage[:, at, :] = jnp.zeros((rows, cols), F32)
     snd_e[...] = ens_stage[...].astype(BF16)
 
-    for load in loads[2:]:
+    ens_copies = all_to_all(snd_e, rcv_e, e_send, e_recv)
+    for load in loads[8:]:
         load.wait()
-    pitch = -(-tile_rows // 8) * 8
-    nx = cols * parts
-    first = group * tile_rows
-    row = jnp.zeros_like(cell)
-    cells = cell[...]
-    for r in range(1, tile_rows):
-        row = row + jnp.where(cells >= (first + r) * nx, 1, 0)
-    col = cells - (first + row) * nx - part * cols
-    slot = step[...] * pitch + row
-    observations = cells.shape[1]
-    in_col = (lax.broadcasted_iota(jnp.int32, (cols, observations), 0) == col).astype(F32).astype(BF16)
-    in_slot = lax.broadcasted_iota(jnp.int32, (3 * pitch, observations), 0) == slot
-    obs_weight = weight[...]
-    values = jnp.concatenate([
-        jnp.where(in_slot, obs_weight, 0.0), jnp.where(in_slot, obs_weight * innovation[...], 0.0)
-    ], axis=0)
-    hi, lo = split2(values)
-    summed = dot(hi, in_col, ((1,), (1,))) + dot(lo, in_col, ((1,), (1,)))
-    for v in range(3):
-        fields[v] = std[v] * control[v]
-    for f in range(6):
-        fields[3 + f] = summed[f * pitch : f * pitch + tile_rows]
-    haloed = (0, 1, 2, 4, 5, 7, 8)
-    lane = lax.broadcasted_iota(jnp.int32, (tile_rows, LANES), 1)
-    packed = jnp.zeros((tile_rows, LANES), F32)
-    for e, f in enumerate(haloed):
-        ends = jnp.where(lane < LANES // 2, fields[f, :, :LANES], fields[f, :, cols - LANES :])
-        window = (lane >= 2 * HALO * e) & (lane < 2 * HALO * (e + 1))
-        packed = jnp.where(window, pltpu.roll(ends, (2 * HALO * e + HALO) % LANES, 1), packed)
-    edge[...] = packed
-
     count = spectrum.shape[1]
     inner = count // parts
     wave = lax.broadcasted_iota(jnp.int32, (SLOTS * (-(-residues // SLOTS)), count), 1)
@@ -234,42 +224,6 @@
     f_hi, f_lo = split2(forward)
     b_hi, b_lo = split2(backward)
     waves[...] = dot(f_hi, ahead) + dot(f_lo, ahead) + dot(b_hi, behind) + dot(b_lo, behind)
-
-    pl.semaphore_wait(barrier, groups * parts - 1)
-
-    def all_to_all(source, target, send, recv):
-        copies = []
-        for i in range(1, parts):
-            to = lax.rem(part + i, parts)
-            copies.append(pltpu.make_async_remote_copy(
-                src_ref=source.at[to], dst_ref=target.at[part],
-                send_sem=send.at[i], recv_sem=recv.at[i], device_id={"sp": to},
-            ))
-            copies[-1].start()
-        target[part] = source[part]
-        started.extend(copies)
-        return copies
-
-    def received(copies):
-        for copy in copies:
-            copy.wait_recv()
-
-    alpha_copies = all_to_all(snd_a, rcv_a, a_send, a_recv)
-    ens_copies = all_to_all(snd_e, rcv_e, e_send, e_recv)
-    field_copies = []
-    for j in range(groups):
-        to = lax.rem(group + j, groups)
-        plans = [(1, right, edge, rcv_edge.at[0, group]), (2, left, edge, rcv_edge.at[1, group])]
-        if j > 0:
-            plans.append((0, part, fields, rcv_f.at[group]))
-        for kind, at, source, target in plans:
-            field_copies.append(pltpu.make_async_remote_copy(
-                src_ref=source, dst_ref=target,
-                send_sem=f_send.at[kind, j], recv_sem=f_recv.at[kind, j], device_id={"grp": to, "sp": at},
-            ))
-            field_copies[-1].start()
-    started.extend(field_copies)
-    rcv_f[group] = fields[...]
 
     def filtered(xs):
         pieces = [[x[:, h * LANES : (h + 1) * LANES] for x in xs] for h in range(halves)]
@@ -313,6 +267,54 @@
 
     received(alpha_copies)
     localized = filtered([rcv_a[p].astype(F32) for p in range(parts)])
+    for load in loads[2:8]:
+        load.wait()
+    pitch = -(-tile_rows // 8) * 8
+    nx = cols * parts
+    first = group * tile_rows
+    row = jnp.zeros_like(cell)
+    cells = cell[...]
+    for r in range(1, tile_rows):
+        row = row + jnp.where(cells >= (first + r) * nx, 1, 0)
+    col = cells - (first + row) * nx - part * cols
+    slot = step[...] * pitch + row
+    observations = cells.shape[1]
+    in_col = (lax.broadcasted_iota(jnp.int32, (cols, observations), 0) == col).astype(F32).astype(BF16)
+    in_slot = lax.broadcasted_iota(jnp.int32, (3 * pitch, observations), 0) == slot
+    obs_weight = weight[...]
+    values = jnp.concatenate([
+        jnp.where(in_slot, obs_weight, 0.0), jnp.where(in_slot, obs_weight * innovation[...], 0.0)
+    ], axis=0)
+    hi, lo = split2(values)
+    summed = dot(hi, in_col, ((1,), (1,))) + dot(lo, in_col, ((1,), (1,)))
+    for v in range(3):
+        fields[v] = std[v] * control[v]
+    for f in range(6):
+        fields[3 + f] = summed[f * pitch : f * pitch + tile_rows]
+    haloed = (0, 1, 2, 4, 5, 7, 8)
+    lane = lax.broadcasted_iota(jnp.int32, (tile_rows, LANES), 1)
+    packed = jnp.zeros((tile_rows, LANES), F32)
+    for e, f in enumerate(haloed):
+        ends = jnp.where(lane < LANES // 2, fields[f, :, :LANES], fields[f, :, cols - LANES :])
+        window = (lane >= 2 * HALO * e) & (lane < 2 * HALO * (e + 1))
+        packed = jnp.where(window, pltpu.roll(ends, (2 * HALO * e + HALO) % LANES, 1), packed)
+    edge[...] = packed
+
+    field_copies = []
+    for j in range(groups):
+        to = lax.rem(group + j, groups)
+        plans = [(1, right, edge, rcv_edge.at[0, group]), (2, left, edge, rcv_edge.at[1, group])]
+        if j > 0:
+            plans.append((0, part, fields, rcv_f.at[group]))
+        for kind, at, source, target in plans:
+            field_copies.append(pltpu.make_async_remote_copy(
+                src_ref=source, dst_ref=target,
+                send_sem=f_send.at[kind, j], recv_sem=f_recv.at[kind, j], device_id={"grp": to, "sp": at},
+            ))
+            field_copies[-1].start()
+    started.extend(field_copies)
+    rcv_f[group] = fields[...]
+
     received(ens_copies)
     at_slot = lax.broadcasted_iota(jnp.int32, (SLOTS, cols), 0)
     firsts, seconds = [], []
@@ -462,7 +464,7 @@
             jax.ShapeDtypeStruct(alpha.shape, F32),
             jax.ShapeDtypeStruct(control.shape, F32),
         ),
-        in_specs=[ANY] * len(operands),
+        in_specs=[HBM] * len(operands),
         out_specs=(vmem, vmem),
         scratch_shapes=[
             *[pltpu.VMEM(t.shape, t.dtype) for t in operands],
@@ -485,7 +487,7 @@
             dma((parts,)), dma((parts,)), dma((parts,)), dma((parts,)),
             dma((3, groups)), dma((3, groups)),
         ],
-        compiler_params=pltpu.CompilerParams(collective_id=0, has_side_effects=True, vmem_limit_bytes=40 << 20),
+        compiler_params=pltpu.CompilerParams(collective_id=0, has_side_effects=True, vmem_limit_bytes=66700000),
     )(*operands)
     return corr, grad_control
 

time: 50.2 us -> 38.6 us (0.77); the launches traced: 49.5 us -> 38.4 us
  local copies, waits for them, and re-layouts: 14.1 us -> 2.21 us
  Pallas kernels: 34.7 us -> 35.6 us
    unnamed x34 -> x4, local copies, waits for them, and re-layouts: 14.1 us -> 2.21 us
    pallas_call x1, Pallas kernels: 34.7 us -> 35.6 us  [per_device(): pl.pallas_call(functools.partial(kernel, groups, parts, spread), out_shap...]
where the time goes in v2:
time: 38.6 us; the launch traced here: 38.4 us
  Pallas kernels  35.6 us (92%)
  local copies, waits for them, and re-layouts  2.21 us (6%)
  between operations  0.65 us (2%)
    pallas_call x1, Pallas kernels, per_device(): pl.pallas_call(functools.partial(kernel, groups, parts, spread), out_shap...  35.6 us
    unnamed x4, local copies, waits for them, and re-layouts  2.21 us

profile of v2, /device:TPU:0, one launch (start us, length us, event | category | flops | bytes accessed | tf_op | source)
XLA Modules:
  0.0 38.4 jit_solution(13952156275570160892)
XLA Ops:
  0.6 35.6 %shard_map.167 = (f32[10,16,256]{2,1,0:T(8,128)}, f32[3,8,256]{2,1,0:T(8,128)}) custom-call(f32[10,16,256]{2,1,0:T(8,128)} %alpha_any.1, bf16[10,3,16,256]{3,2,1,0:T(8,128)(2,1)} %ens_any.1, f32[3,8,256]{2,1,0:T(8,128)} %std_any.1, f32[3,8,256]{2,1,0:T(8,128)} %control_any.1, f32[1,1024]{1,0:T(1,128)} %bitcast.5, s32[1,1024]{1,0:T(1,128)} %bitcast.6, ...), custom_call_target="tpu_custom_call" | custom-call | tf_op jit(solution)/shard_map/pallas_call | solution.py:461
  36.2 0.0 copy-start
  36.2 1.6 %copy.20 = f32[10,16,256]{2,1,0:T(8,128)} copy(f32[10,16,256]{2,1,0:T(8,128)} %get-tuple-element.4) | data formatting | bytes 327680
  37.8 0.0 copy-done
  37.8 0.6 %copy.21 = f32[3,8,256]{2,1,0:T(8,128)} copy(f32[3,8,256]{2,1,0:T(8,128)S(1)} %copy-done) | data formatting | bytes 49152
Async XLA Ops:
  36.2 1.6 %copy-start = (f32[3,8,256]{2,1,0:T(8,128)S(1)}, f32[3,8,256]{2,1,0:T(8,128)}, u32[]{:S(2)}) copy-start(f32[3,8,256]{2,1,0:T(8,128)} %get-tuple-element.5) | copy-start | bytes 73732

commit v3 on v2

--- a/solution.py
+++ b/solution.py
@@ -136,8 +136,8 @@
     alpha, ens, std, control, spectrum, cell, step, innovation, weight,
     fwd_hi, fwd_lo, inv_hi, inv_lo, tw_c, tw_s, pick,
     stage, ens_stage, adjoint, waves, fields, wide,
-    snd_a, rcv_a, snd_e, rcv_e, snd_i, rcv_i, snd_h, rcv_h, snd_o, rcv_o, rcv_f, edge, rcv_edge,
-    load_sem, a_send, a_recv, e_send, e_recv, i_send, i_recv, h_send, h_recv, o_send, o_recv, f_send, f_recv,
+    snd_a, rcv_a, snd_e, rcv_e, message, snd_i, rcv_i, snd_h, rcv_h, snd_o, rcv_o, rcv_f, edge, rcv_edge,
+    load_sem, a_send, a_recv, e_send, e_recv, i_send, i_recv, h_send, h_recv, o_send, o_recv, f_send, f_recv, whole,
 ):
     group, part = lax.axis_index("grp"), lax.axis_index("sp")
     left, right = lax.rem(part + parts - 1, parts), lax.rem(part + 1, parts)
@@ -151,11 +151,10 @@
     started = []
 
     barrier = pltpu.get_barrier_semaphore()
-    for j in range(groups):
-        for i in range(parts):
-            if i + j > 0:
-                device = {"grp": lax.rem(group + j, groups), "sp": lax.rem(part + i, parts)}
-                pl.semaphore_signal(barrier, inc=1, device_id=device)
+    for i in range(1, parts):
+        pl.semaphore_signal(barrier, inc=1, device_id={"sp": lax.rem(part + i, parts)})
+    for j in range(1, groups):
+        pl.semaphore_signal(barrier, inc=1, device_id={"grp": lax.rem(group + j, groups)})
 
     pairs = [
         (alpha_any, alpha), (ens_any, ens), (cell_any, cell), (step_any, step), (innovation_any, innovation),
@@ -168,105 +167,12 @@
         load.start()
 
     loads[0].wait()
+    if stage.shape[1] > halves * members:
+        stage[:, halves * members :, :] = jnp.zeros((rows, stage.shape[1] - halves * members, LANES), F32)
     for m in range(members):
-        stage[:, m, :] = alpha[m]
-    for m in range(SLOTS - members):
-        stage[:, members + m, :] = alpha[m] if m < spare else jnp.zeros((rows, cols), F32)
+        for h in range(halves):
+            stage[:, h * members + m, :] = alpha[m, :, h * LANES : (h + 1) * LANES]
     snd_a[...] = stage[...].astype(BF16)
-    def all_to_all(source, target, send, recv):
-        copies = []
-        for i in range(1, parts):
-            to = lax.rem(part + i, parts)
-            copies.append(pltpu.make_async_remote_copy(
-                src_ref=source.at[to], dst_ref=target.at[part],
-                send_sem=send.at[i], recv_sem=recv.at[i], device_id={"sp": to},
-            ))
-            copies[-1].start()
-        target[part] = source[part]
-        started.extend(copies)
-        return copies
-
-    def received(copies):
-        for copy in copies:
-            copy.wait_recv()
-
-    pl.semaphore_wait(barrier, groups * parts - 1)
-
-    alpha_copies = all_to_all(snd_a, rcv_a, a_send, a_recv)
-    loads[1].wait()
-    used = set()
-    for v in range(3):
-        for m in range(members):
-            at = slot_of(v, m, members)
-            used.add(at)
-            ens_stage[:, at, :] = ens[m, v].astype(F32)
-    for at in range(2 * SLOTS):
-        if at not in used:
-            ens_stage[:, at, :] = jnp.zeros((rows, cols), F32)
-    snd_e[...] = ens_stage[...].astype(BF16)
-
-    ens_copies = all_to_all(snd_e, rcv_e, e_send, e_recv)
-    for load in loads[8:]:
-        load.wait()
-    count = spectrum.shape[1]
-    inner = count // parts
-    wave = lax.broadcasted_iota(jnp.int32, (SLOTS * (-(-residues // SLOTS)), count), 1)
-    residue = lax.broadcasted_iota(jnp.int32, wave.shape, 0)
-    weights = jnp.broadcast_to(spectrum[...], wave.shape)
-    forward = jnp.where((lax.rem(wave, parts) == residue) & (residue < residues), weights, 0.0)
-    mirrored = (lax.rem(wave + residue, parts) == 0) & (residue > 0) & (residue < residues - 1)
-    backward = jnp.where(mirrored, weights, 0.0)
-    k = lax.broadcasted_iota(jnp.int32, (count, 4 * inner), 0)
-    j = lax.rem(lax.broadcasted_iota(jnp.int32, (count, 4 * inner), 1), 2 * inner)
-    ahead, behind = k - parts * (j - inner), k - parts * (inner - 1 - j)
-    ahead = jnp.where((ahead >= 0) & (ahead < parts), 1.0, 0.0).astype(BF16)
-    behind = jnp.where((behind >= 0) & (behind < parts), 1.0, 0.0).astype(BF16)
-    f_hi, f_lo = split2(forward)
-    b_hi, b_lo = split2(backward)
-    waves[...] = dot(f_hi, ahead) + dot(f_lo, ahead) + dot(b_hi, behind) + dot(b_lo, behind)
-
-    def filtered(xs):
-        pieces = [[x[:, h * LANES : (h + 1) * LANES] for x in xs] for h in range(halves)]
-        spectra = [real_dft(piece) for piece in pieces]
-        res, ims = [], []
-        for k1 in range(residues):
-            parts_re, parts_im = [], []
-            for h in range(halves):
-                c = tw_c[k1 : k1 + 1, h * LANES : (h + 1) * LANES]
-                s = tw_s[k1 : k1 + 1, h * LANES : (h + 1) * LANES]
-                re, im = spectra[h][k1]
-                if k1 == 0:
-                    parts_re.append(re)
-                    parts_im.append(jnp.zeros_like(re))
-                elif im is None:
-                    parts_re.append(re * c)
-                    parts_im.append(-re * s)
-                else:
-                    parts_re.append(re * c + im * s)
-                    parts_im.append(im * c - re * s)
-            res.append(jnp.concatenate(parts_re + parts_im, axis=1))
-        y_hi, y_lo = split2(jnp.concatenate(res, axis=0))
-        z = dot(y_hi, fwd_hi[...]) + dot(y_lo, fwd_hi[...]) + dot(y_hi, fwd_lo[...])
-        z = jnp.concatenate(
-            [z[k1 * SLOTS : (k1 + 1) * SLOTS] * waves[k1 : k1 + 1, :] for k1 in range(residues)], axis=0
-        )
-        z_hi, z_lo = split2(z)
-        v = dot(z_hi, inv_hi[...]) + dot(z_lo, inv_hi[...]) + dot(z_hi, inv_lo[...])
-        outs = []
-        for h in range(halves):
-            zs = []
-            for k1 in range(residues):
-                c = tw_c[k1 : k1 + 1, h * LANES : (h + 1) * LANES]
-                s = tw_s[k1 : k1 + 1, h * LANES : (h + 1) * LANES]
-                at = slice(k1 * SLOTS, (k1 + 1) * SLOTS)
-                re = v[at, h * LANES : (h + 1) * LANES]
-                im = v[at, cols + h * LANES : cols + (h + 1) * LANES]
-                zs.append((re, im) if k1 == 0 else (re * c - im * s, im * c + re * s))
-            outs.append(real_sum(zs, parts))
-        return [jnp.concatenate([outs[h][p] for h in range(halves)], axis=1) for p in range(parts)]
-
-    received(alpha_copies)
-    localized = filtered([rcv_a[p].astype(F32) for p in range(parts)])
     for load in loads[2:8]:
         load.wait()
     pitch = -(-tile_rows // 8) * 8
@@ -300,6 +206,43 @@
         packed = jnp.where(window, pltpu.roll(ends, (2 * HALO * e + HALO) % LANES, 1), packed)
     edge[...] = packed
 
+    def all_to_all(source, target, send, recv):
+        copies = []
+        for i in range(1, parts):
+            to = lax.rem(part + i, parts)
+            copies.append(pltpu.make_async_remote_copy(
+                src_ref=source.at[to], dst_ref=target.at[part],
+                send_sem=send.at[i], recv_sem=recv.at[i], device_id={"sp": to},
+            ))
+            copies[-1].start()
+        target[part] = source[part]
+        started.extend(copies)
+        return copies
+
+    def received(copies):
+        for copy in copies:
+            copy.wait_recv()
+
+    pl.semaphore_wait(barrier, parts + groups - 2)
+    for j in range(1, groups):
+        pl.semaphore_signal(whole, inc=1, device_id={"grp": lax.rem(group + j, groups)})
+
+    alpha_copies = all_to_all(snd_a, rcv_a, a_send, a_recv)
+    loads[1].wait()
+    used = set()
+    for v in range(3):
+        for m in range(members):
+            at = slot_of(v, m, members)
+            used.add(at)
+            ens_stage[:, at, :] = ens[m, v].astype(F32)
+    for at in range(2 * SLOTS):
+        if at not in used:
+            ens_stage[:, at, :] = jnp.zeros((rows, cols), F32)
+    snd_e[...] = ens_stage[...].astype(BF16)
+
+    ens_copies = all_to_all(snd_e, rcv_e, e_send, e_recv)
+    if groups > 1:
+        pl.semaphore_wait(whole, groups - 1)
     field_copies = []
     for j in range(groups):
         to = lax.rem(group + j, groups)
@@ -315,13 +258,80 @@
     started.extend(field_copies)
     rcv_f[group] = fields[...]
 
+    for load in loads[8:]:
+        load.wait()
+    count = spectrum.shape[1]
+    inner = count // parts
+    wave = lax.broadcasted_iota(jnp.int32, (SLOTS * (-(-residues // SLOTS)), count), 1)
+    residue = lax.broadcasted_iota(jnp.int32, wave.shape, 0)
+    weights = jnp.broadcast_to(spectrum[...], wave.shape)
+    forward = jnp.where((lax.rem(wave, parts) == residue) & (residue < residues), weights, 0.0)
+    mirrored = (lax.rem(wave + residue, parts) == 0) & (residue > 0) & (residue < residues - 1)
+    backward = jnp.where(mirrored, weights, 0.0)
+    k = lax.broadcasted_iota(jnp.int32, (count, 4 * inner), 0)
+    j = lax.rem(lax.broadcasted_iota(jnp.int32, (count, 4 * inner), 1), 2 * inner)
+    ahead, behind = k - parts * (j - inner), k - parts * (inner - 1 - j)
+    ahead = jnp.where((ahead >= 0) & (ahead < parts), 1.0, 0.0).astype(BF16)
+    behind = jnp.where((behind >= 0) & (behind < parts), 1.0, 0.0).astype(BF16)
+    f_hi, f_lo = split2(forward)
+    b_hi, b_lo = split2(backward)
+    waves[...] = dot(f_hi, ahead) + dot(f_lo, ahead) + dot(b_hi, behind) + dot(b_lo, behind)
+
+    def filtered(xs):
+        pieces = xs
+        spectra = [real_dft(piece) for piece in pieces]
+        res, ims = [], []
+        for k1 in range(residues):
+            parts_re, parts_im = [], []
+            for h in range(halves):
+                c = tw_c[k1 : k1 + 1, h * LANES : (h + 1) * LANES]
+                s = tw_s[k1 : k1 + 1, h * LANES : (h + 1) * LANES]
+                re, im = spectra[h][k1]
+                if k1 == 0:
+                    parts_re.append(re)
+                    parts_im.append(jnp.zeros_like(re))
+                elif im is None:
+                    parts_re.append(re * c)
+                    parts_im.append(-re * s)
+                else:
+                    parts_re.append(re * c + im * s)
+                    parts_im.append(im * c - re * s)
+            res.append(jnp.concatenate(parts_re + parts_im, axis=1))
+        y_hi, y_lo = split2(jnp.concatenate(res, axis=0))
+        z = dot(y_hi, fwd_hi[...]) + dot(y_lo, fwd_hi[...]) + dot(y_hi, fwd_lo[...])
+        z = jnp.concatenate(
+            [z[k1 * SLOTS : (k1 + 1) * SLOTS] * waves[k1 : k1 + 1, :] for k1 in range(residues)], axis=0
+        )
+        z_hi, z_lo = split2(z)
+        v = dot(z_hi, inv_hi[...]) + dot(z_lo, inv_hi[...]) + dot(z_hi, inv_lo[...])
+        outs = []
+        for h in range(halves):
+            zs = []
+            for k1 in range(residues):
+                c = tw_c[k1 : k1 + 1, h * LANES : (h + 1) * LANES]
+                s = tw_s[k1 : k1 + 1, h * LANES : (h + 1) * LANES]
+                at = slice(k1 * SLOTS, (k1 + 1) * SLOTS)
+                re = v[at, h * LANES : (h + 1) * LANES]
+                im = v[at, cols + h * LANES : cols + (h + 1) * LANES]
+                zs.append((re, im) if k1 == 0 else (re * c - im * s, im * c + re * s))
+            outs.append(real_sum(zs, parts))
+        return outs
+
+    received(alpha_copies)
+    came = [[None] * parts for _ in range(halves)]
+    for p in range(parts):
+        x = rcv_a[p].astype(F32)
+        for h in range(halves):
+            came[h][p] = (x if h == 0 else pltpu.roll(x, x.shape[0] - h * members, 0))[:SLOTS]
+    localized = filtered(came)
     received(ens_copies)
     at_slot = lax.broadcasted_iota(jnp.int32, (SLOTS, cols), 0)
     firsts, seconds = [], []
     for p in range(parts):
-        loc = localized[p].astype(BF16).astype(F32)
+        loc = jnp.concatenate([localized[h][p] for h in range(halves)], axis=1).astype(BF16).astype(F32)
         moved = jnp.where(at_slot < members, loc, pltpu.roll(loc, shift, 0)) if shift else loc
-        firsts.append(rcv_e[p, :SLOTS].astype(F32) * loc)
+        again = jnp.where(at_slot < members, loc, pltpu.roll(loc, members, 0))
+        firsts.append(rcv_e[p, :SLOTS].astype(F32) * again)
         seconds.append(rcv_e[p, SLOTS:].astype(F32) * moved)
     a_hi, a_lo = split2(jnp.concatenate(firsts, axis=0))
     b_hi, b_lo = split2(jnp.concatenate(seconds, axis=0))
@@ -332,12 +342,13 @@
     for v in range(3):
         field = inc[v * parts : (v + 1) * parts]
         for h in range(halves):
-            snd_i[:, v * halves + h, :] = field[:, h * LANES : (h + 1) * LANES]
+            message[:, v * halves + h, :] = field[:, h * LANES : (h + 1) * LANES]
         after = pltpu.roll(field[:, :LANES], parts - 1, 0)
         before = pltpu.roll(field[:, cols - LANES :], 1, 0)
         ends = pltpu.roll(jnp.where(lane < LANES // 2, after, before), 2 * HALO * v + HALO, 1)
         packed = jnp.where((lane >= 2 * HALO * v) & (lane < 2 * HALO * (v + 1)), ends, packed)
-    snd_i[:, 3 * halves, :] = packed
+    message[:, 3 * halves, :] = packed
+    snd_i[...] = message[...].astype(BF16)
     copies = []
     for i in range(parts):
         for j in range(groups):
@@ -366,11 +377,13 @@
 
     received(copies)
 
+    total = rcv_i[0].astype(F32)
+    for g in range(1, groups):
+        total = total + rcv_i[g].astype(F32)
+    message[...] = total
+
     def gathered(index):
-        total = rcv_i[0, :, index, :]
-        for g in range(1, groups):
-            total = total + rcv_i[g, :, index, :]
-        return total
+        return message[:, index, :]
 
     ends = gathered(3 * halves)
     state0 = []
@@ -391,17 +404,19 @@
         adjoint[v] = field
         half = field.astype(BF16).astype(F32)
         for h in range(halves):
-            snd_h[:, v * halves + h, :] = half[:, h * LANES : (h + 1) * LANES]
+            message[:, v * halves + h, :] = half[:, h * LANES : (h + 1) * LANES]
+    snd_h[...] = message[...].astype(BF16)
     copies = all_to_all(snd_h, rcv_h, h_send, h_recv)
     for v in range(3):
         grad_control_ref[v] = control[v] + std[v] * adjoint[v, tile, :]
     received(copies)
     weighted = []
     for p in range(parts):
+        came_h = rcv_h[p].astype(F32)
         halfs = []
         for v in range(3):
             pieces = [
-                jnp.broadcast_to(rcv_h[p, v * halves + h : v * halves + h + 1, :], (SLOTS, LANES)) for h in range(halves)
+                jnp.broadcast_to(came_h[v * halves + h : v * halves + h + 1], (SLOTS, LANES)) for h in range(halves)
             ]
             halfs.append(jnp.concatenate(pieces, axis=1))
         a = rcv_e[p, :SLOTS].astype(F32) * jnp.where(at_slot < members, halfs[0], halfs[2])
@@ -410,15 +425,30 @@
         if shift:
             own = jnp.where((at_slot >= spare) & (at_slot < members), pltpu.roll(b, SLOTS - shift, 0), own)
         weighted.append(a + b + own)
-    outs = filtered(weighted)
+    outs = filtered([[x[:, h * LANES : (h + 1) * LANES] for x in weighted] for h in range(halves)])
     for p in range(parts):
-        snd_o[p] = outs[p].astype(BF16)
+        for h in range(halves):
+            stage[p, h * members : (h + 1) * members, :] = outs[h][p][:members]
+        snd_o[p] = stage[p].astype(BF16)
     received(all_to_all(snd_o, rcv_o, o_send, o_recv))
     stage[...] = rcv_o[...].astype(F32)
     for m in range(members):
-        corr_ref[m] = alpha[m] + spread * stage[:, m, :]
+        for h in range(halves):
+            at = slice(h * LANES, (h + 1) * LANES)
+            corr_ref[m, :, at] = alpha[m, :, at] + spread * stage[:, h * members + m, :]
     for copy in started:
         copy.wait_send()
+
+
+def finish(corr_ref, grad_control_ref, corr_out, grad_control_out, sem):
+    copies = [
+        pltpu.make_async_copy(corr_ref, corr_out, sem.at[0]),
+        pltpu.make_async_copy(grad_control_ref, grad_control_out, sem.at[1]),
+    ]
+    for copy in copies:
+        copy.start()
+    for copy in copies:
+        copy.wait()
 
 
 def tables(parts, cols, waves, members):
@@ -455,30 +485,32 @@
         obs_cell[None], obs_step[None], innovation[None], obs_weight[None],
         *tables(parts, cols, loc_spectrum.shape[0], members),
     )
+    packed = (8 * (-(-max(cols // LANES * members, SLOTS) // 8)), LANES)
     message = (8 * (-(-(3 * cols // LANES + 1) // 8)), LANES)
     vmem = pl.BlockSpec(memory_space=pltpu.VMEM)
     dma = pltpu.SemaphoreType.DMA
     corr, grad_control = pl.pallas_call(
         functools.partial(kernel, groups, parts, spread),
         out_shape=(
-            jax.ShapeDtypeStruct(alpha.shape, F32),
-            jax.ShapeDtypeStruct(control.shape, F32),
+            pltpu.VMEM(alpha.shape, F32),
+            pltpu.VMEM(control.shape, F32),
         ),
         in_specs=[HBM] * len(operands),
         out_specs=(vmem, vmem),
         scratch_shapes=[
             *[pltpu.VMEM(t.shape, t.dtype) for t in operands],
-            pltpu.VMEM((rows, SLOTS, cols), F32),
+            pltpu.VMEM((rows, *packed), F32),
             pltpu.VMEM((rows, 2 * SLOTS, cols), F32),
             pltpu.VMEM((3, rows, cols), F32),
             pltpu.VMEM((SLOTS * (-(-residues // SLOTS)), 4 * inner), F32),
             pltpu.VMEM((9, tile_rows, cols), F32),
             pltpu.VMEM((9, rows, cols + LANES), F32),
-            pltpu.VMEM((parts, SLOTS, cols), BF16), pltpu.VMEM((parts, SLOTS, cols), BF16),
+            pltpu.VMEM((parts, *packed), BF16), pltpu.VMEM((parts, *packed), BF16),
             pltpu.VMEM((parts, 2 * SLOTS, cols), BF16), pltpu.VMEM((parts, 2 * SLOTS, cols), BF16),
-            pltpu.VMEM((parts, *message), F32), pltpu.VMEM((groups, parts, *message), F32),
-            pltpu.VMEM((parts, *message), F32), pltpu.VMEM((parts, *message), F32),
-            pltpu.VMEM((parts, SLOTS, cols), BF16), pltpu.VMEM((parts, SLOTS, cols), BF16),
+            pltpu.VMEM((parts, *message), F32),
+            pltpu.VMEM((parts, *message), BF16), pltpu.VMEM((groups, parts, *message), BF16),
+            pltpu.VMEM((parts, *message), BF16), pltpu.VMEM((parts, *message), BF16),
+            pltpu.VMEM((parts, *packed), BF16), pltpu.VMEM((parts, *packed), BF16),
             pltpu.VMEM((groups, 9, tile_rows, cols), F32),
             pltpu.VMEM((tile_rows, LANES), F32), pltpu.VMEM((2, groups, tile_rows, LANES), F32),
             dma((len(operands),)),
@@ -486,10 +518,18 @@
             dma((parts, groups)), dma((parts, groups)),
             dma((parts,)), dma((parts,)), dma((parts,)), dma((parts,)),
             dma((3, groups)), dma((3, groups)),
+            pltpu.SemaphoreType.REGULAR,
         ],
-        compiler_params=pltpu.CompilerParams(collective_id=0, has_side_effects=True, vmem_limit_bytes=66700000),
+        compiler_params=pltpu.CompilerParams(collective_id=0, has_side_effects=True, vmem_limit_bytes=63 << 20),
     )(*operands)
-    return corr, grad_control
+    return pl.pallas_call(
+        finish,
+        out_shape=(jax.ShapeDtypeStruct(alpha.shape, F32), jax.ShapeDtypeStruct(control.shape, F32)),
+        in_specs=[vmem] * 2,
+        out_specs=(HBM, HBM),
+        scratch_shapes=[dma((2,))],
+        compiler_params=pltpu.CompilerParams(vmem_limit_bytes=1 << 20),
+    )(corr, grad_control)
 
 
 def solution(mesh):

time: 38.6 us -> 35 us (0.907)
  local copies, waits for them, and re-layouts: 2.21 us -> 0 us
  Pallas kernels: 35.6 us -> 34.3 us
    unnamed x4 -> x0, local copies, waits for them, and re-layouts: 2.21 us -> none
    pallas_call x1, Pallas kernels: 35.6 us -> 33.6 us  [per_device(): pl.pallas_call(functools.partial(kernel, groups, parts, spread), out_shap...]
    pallas_call x0 -> x1, Pallas kernels: none -> 0.69 us  [per_device(): pl.pallas_call(finish, out_shape=(jax.ShapeDtypeStruct(alpha.shape, F32),...]
where the time goes in v3:
time: 35 us; the launch traced here: 34.9 us
  Pallas kernels  34.3 us (98%)
  between operations  0.64 us (2%)
    pallas_call x1, Pallas kernels, per_device(): pl.pallas_call(functools.partial(kernel, groups, parts, spread), out_shap...  33.6 us

profile of v3, /device:TPU:0, one launch (start us, length us, event | category | flops | bytes accessed | tf_op | source)
XLA Modules:
  0.0 34.9 jit_solution(3005701636394207148)
XLA Ops:
  0.6 33.6 %shard_map.167 = (f32[10,16,256]{2,1,0:T(8,128)S(1)}, f32[3,8,256]{2,1,0:T(8,128)S(1)}) custom-call(f32[10,16,256]{2,1,0:T(8,128)} %alpha_any.1, bf16[10,3,16,256]{3,2,1,0:T(8,128)(2,1)} %ens_any.1, f32[3,8,256]{2,1,0:T(8,128)} %std_any.1, f32[3,8,256]{2,1,0:T(8,128)} %control_any.1, f32[1,1024]{1,0:T(1,128)} %bitcast.5, s32[1,1024]{1,0:T(1,128)} %bitcast.6, ...), custom_call_target="tpu_custom_call" | custom-call | tf_op jit(solution)/shard_map/pallas_call | solution.py:492
  34.2 0.7 %shard_map.168 = (f32[10,16,256]{2,1,0:T(8,128)}, f32[3,8,256]{2,1,0:T(8,128)}) custom-call(f32[10,16,256]{2,1,0:T(8,128)S(1)} %get-tuple-element.4.corr_ref, f32[3,8,256]{2,1,0:T(8,128)S(1)} %get-tuple-element.5.grad_control_ref), custom_call_target="tpu_custom_call" | custom-call | tf_op jit(solution)/shard_map/pallas_call | solution.py:525

commit v4 on v3

v4 whole, which is shorter than its diff:
```python
import functools
import math

import jax
import jax.numpy as jnp
import numpy as np
from jax import lax
from jax.experimental import pallas as pl
from jax.experimental.pallas import tpu as pltpu
from jax.sharding import PartitionSpec as P

COURANT = 0.4
LANES = 128
HALO = 8
BATCHES = 4
BF16, F32 = jnp.bfloat16, jnp.float32
HBM = pl.BlockSpec(memory_space=pltpu.HBM)


def dot(a, b, contract=((1,), (0,))):
    return lax.dot_general(a, b, (contract, ((), ())), preferred_element_type=F32)


def split2(x):
    hi = x.astype(BF16)
    return hi, (x - hi.astype(F32)).astype(BF16)


def both(table):
    table = np.asarray(table, np.float32)
    hi = table.astype(BF16)
    return hi, (table - hi.astype(np.float32)).astype(BF16)


def add(a, b, sign=1.0):
    re = a[0] + b[0] if sign > 0 else a[0] - b[0]
    if b[1] is None:
        return re, a[1]
    if a[1] is None:
        return re, b[1] if sign > 0 else -b[1]
    return re, a[1] + b[1] if sign > 0 else a[1] - b[1]


def conj(a):
    return a[0], None if a[1] is None else -a[1]


def turn(a, eighths, n):
    at = (eighths % n) / n
    if at == 0:
        return a
    re, im = a
    if at == 0.25:
        return (jnp.zeros_like(re) if im is None else -im), re
    if at == 0.75:
        return (jnp.zeros_like(re) if im is None else im), -re
    c, s = math.cos(2 * math.pi * at), math.sin(2 * math.pi * at)
    if im is None:
        return c * re, s * re
    return c * re - s * im, c * im + s * re


def real_dft(xs):
    n = len(xs)
    if n == 1:
        return [(xs[0], None)]
    if n == 2:
        return [(xs[0] + xs[1], None), (xs[0] - xs[1], None)]
    half = n // 2
    even, odd = real_dft(xs[0::2]), real_dft(xs[1::2])
    out = [None] * (half + 1)
    for k in range(half // 2 + 1):
        t = turn(odd[k], -k, n)
        out[k] = add(even[k], t)
        if half - k != k:
            out[half - k] = conj(add(even[k], t, -1.0))
    return out


def real_sum(zs, n):
    if n == 1:
        return [zs[0][0]]
    if n == 2:
        return [zs[0][0] + zs[1][0], zs[0][0] - zs[1][0]]
    half = n // 2
    even, odd = [], []
    for k in range(half // 2 + 1):
        if half - k == k:
            even.append(zs[k])
            odd.append(turn(zs[k], k, n))
        else:
            other = conj(zs[half - k])
            even.append(add(zs[k], other))
            odd.append(turn(add(zs[k], other, -1.0), k, n))
    even, odd = real_sum(even, half), real_sum(odd, half)
    return [(even, odd)[p % 2][p // 2] for p in range(n)]


def dx(q):
    width = q.shape[1]
    return 0.5 * (pltpu.roll(q, width - 1, 1) - pltpu.roll(q, 1, 1))


def dy(q):
    rows = q.shape[0]
    at = lax.broadcasted_iota(jnp.int32, q.shape, 0)
    above = jnp.where(at < rows - 1, pltpu.roll(q, rows - 1, 0), 0.0)
    below = jnp.where(at > 0, pltpu.roll(q, 1, 0), 0.0)
    return 0.5 * (above - below)


def model_step(state, rotation):
    h, u, w = state
    h = h - COURANT * (dx(u) + dy(w))
    return h, u - COURANT * dx(h) + rotation * w, w - COURANT * dy(h) - rotation * u


def adjoint_step(state, rotation):
    h, u, w = state
    a = h + COURANT * (dx(u) + dy(w))
    return a, u - rotation * w + COURANT * dx(a), w + rotation * u + COURANT * dy(a)


def round8(n):
    return -(-n // 8) * 8


def layout(members, rows, parts):
    owners = parts // 2
    per = rows // owners
    items = per * members
    slots = round8(items)
    spare = slots - items
    return owners, per, items, slots, spare, 2 * slots + round8(items - 2 * spare)


def slot_of(v, item, items, slots, spare):
    if v < 2:
        return v * slots + item
    if item < spare:
        return items + item
    if item < 2 * spare:
        return slots + items + item - spare
    return 2 * slots + item - 2 * spare


def kernel(
    groups, parts, spread,
    alpha_any, ens_any, std_any, control_any, spectrum_any, cell_any, step_any, innovation_any, weight_any,
    fwd_hi_any, fwd_lo_any, inv_hi_any, inv_lo_any, tw_c_any, tw_s_any, pick_any,
    corr_ref, grad_control_ref,
    alpha, ens, std, control, spectrum, cell, step, innovation, weight,
    fwd_hi, fwd_lo, inv_hi, inv_lo, tw_c, tw_s, pick,
    stage, out_stage, ens_stage, loc_buf, adjoint, waves, fields, wide, message,
    snd_a, rcv_a, snd_e, rcv_e, snd_i, rcv_i, snd_h, rcv_h, snd_o, rcv_o, rcv_f, edge, rcv_edge,
    load_sem, a_send, a_recv, e_send, e_recv, i_send, i_recv, h_send, h_recv, o_send, o_recv, f_send, f_recv, whole,
):
    group, part = lax.axis_index("grp"), lax.axis_index("sp")
    left, right = lax.rem(part + parts - 1, parts), lax.rem(part + 1, parts)
    members, rows, cols = alpha.shape
    tile_rows = control.shape[1]
    tile = pl.ds(pl.multiple_of(group * tile_rows, tile_rows), tile_rows)
    owners, per, items, slots, spare, total_slots = layout(members, rows, parts)
    low = parts // 4
    mine = part - low
    owner = (part >= low) & (part < low + owners)
    halves = cols // LANES
    residues = parts // 2 + 1

    barrier = pltpu.get_barrier_semaphore()
    others = [(0, left), (0, right)] + [(j, at) for j in range(1, groups) for at in (part, left, right)]

    @pl.when(owner)
    def _():
        for i in range(1, parts):
            pl.semaphore_signal(barrier, inc=1, device_id={"sp": lax.rem(part + i, parts)})

    @pl.when(jnp.logical_not(owner))
    def _():
        for i in range(owners):
            pl.semaphore_signal(barrier, inc=1, device_id={"sp": low + lax.rem(part + i, owners)})

    for j, at in others:
        pl.semaphore_signal(barrier, inc=1, device_id={"grp": lax.rem(group + j, groups), "sp": at})

    pairs = [
        (alpha_any, alpha), (ens_any, ens), (cell_any, cell), (step_any, step), (innovation_any, innovation),
        (weight_any, weight), (std_any, std), (control_any, control), (spectrum_any, spectrum),
        (fwd_hi_any, fwd_hi), (fwd_lo_any, fwd_lo), (inv_hi_any, inv_hi), (inv_lo_any, inv_lo),
        (tw_c_any, tw_c), (tw_s_any, tw_s), (pick_any, pick),
    ]
    loads = [pltpu.make_async_copy(a, b, load_sem.at[i]) for i, (a, b) in enumerate(pairs)]
    for load in loads:
        load.start()

    loads[0].wait()
    filled = halves * items
    if stage.shape[1] > filled:
        stage[:, filled:, :] = jnp.zeros((owners, stage.shape[1] - filled, LANES), F32)
    for m in range(members):
        for j in range(per):
            for h in range(halves):
                stage[:, h * items + j * members + m, :] = (
                    alpha[m, j * owners : (j + 1) * owners, h * LANES : (h + 1) * LANES]
                )
    snd_a[...] = stage[...].astype(BF16)

    for load in loads[2:8]:
        load.wait()
    pitch = -(-tile_rows // 8) * 8
    nx = cols * parts
    first = group * tile_rows
    row = jnp.zeros_like(cell)
    cells = cell[...]
    for r in range(1, tile_rows):
        row = row + jnp.where(cells >= (first + r) * nx, 1, 0)
    col = cells - (first + row) * nx - part * cols
    slot = step[...] * pitch + row
    observations = cells.shape[1]
    in_col = (lax.broadcasted_iota(jnp.int32, (cols, observations), 0) == col).astype(F32).astype(BF16)
    in_slot = lax.broadcasted_iota(jnp.int32, (3 * pitch, observations), 0) == slot
    obs_weight = weight[...]
    values = jnp.concatenate([
        jnp.where(in_slot, obs_weight, 0.0), jnp.where(in_slot, obs_weight * innovation[...], 0.0)
    ], axis=0)
    hi, lo = split2(values)
    summed = dot(hi, in_col, ((1,), (1,))) + dot(lo, in_col, ((1,), (1,)))
    for v in range(3):
        fields[v] = std[v] * control[v]
    for f in range(6):
        fields[3 + f] = summed[f * pitch : f * pitch + tile_rows]
    haloed = (0, 1, 2, 4, 5, 7, 8)
    lane = lax.broadcasted_iota(jnp.int32, (tile_rows, LANES), 1)
    packed = jnp.zeros((tile_rows, LANES), F32)
    for e, f in enumerate(haloed):
        ends = jnp.where(lane < LANES // 2, fields[f, :, :LANES], fields[f, :, cols - LANES :])
        window = (lane >= 2 * HALO * e) & (lane < 2 * HALO * (e + 1))
        packed = jnp.where(window, pltpu.roll(ends, (2 * HALO * e + HALO) % LANES, 1), packed)
    edge[...] = packed

    @pl.when(owner)
    def _():
        pl.semaphore_wait(barrier, parts - 1 + len(others))
        for j in range(1, groups):
            pl.semaphore_signal(whole, inc=1, device_id={"grp": lax.rem(group + j, groups)})

    @pl.when(jnp.logical_not(owner))
    def _():
        pl.semaphore_wait(barrier, owners + len(others))

    class ToOwners:
        def __init__(self, source, target, send, recv):
            self.source, self.target, self.send, self.recv = source, target, send, recv

        def copy(self, i):
            at = lax.rem(part + i, owners)
            return low + at, pltpu.make_async_remote_copy(
                src_ref=self.source.at[at], dst_ref=self.target.at[part],
                send_sem=self.send.at[i], recv_sem=self.recv.at[part], device_id={"sp": low + at},
            )

        def start(self):
            for i in range(owners):
                to, copy = self.copy(i)
                pl.when(to != part)(copy.start)

        def take_own(self):
            self.target[part] = self.source[mine]

        def receive(self, i):
            at = lax.rem(part + parts - i, parts)
            pltpu.make_async_remote_copy(
                src_ref=self.source.at[0], dst_ref=self.target.at[at],
                send_sem=self.send.at[0], recv_sem=self.recv.at[at], device_id={"sp": left},
            ).wait_recv()

        def finish(self):
            for i in range(owners):
                to, copy = self.copy(i)
                pl.when(to != part)(copy.wait_send)

    alphas = ToOwners(snd_a, rcv_a, a_send, a_recv)
    enses = ToOwners(snd_e, rcv_e, e_send, e_recv)
    halfs = ToOwners(snd_h, rcv_h, h_send, h_recv)
    alphas.start()
    field_copies = []
    for j in range(groups):
        to = lax.rem(group + j, groups)
        plans = [(1, right, edge, rcv_edge.at[0, group]), (2, left, edge, rcv_edge.at[1, group])]
        if j > 0:
            plans.append((0, part, fields, rcv_f.at[group]))
        for kind, at, source, target in plans:
            field_copies.append(pltpu.make_async_remote_copy(
                src_ref=source, dst_ref=target,
                send_sem=f_send.at[kind, j], recv_sem=f_recv.at[kind, j], device_id={"grp": to, "sp": at},
            ))
            field_copies[-1].start()
    rcv_f[group] = fields[...]


    loads[1].wait()
    used = set()
    for v in range(3):
        for m in range(members):
            field = ens[m, v].astype(F32)
            for j in range(per):
                at = slot_of(v, j * members + m, items, slots, spare)
                used.add(at)
                ens_stage[:, at, :] = field[j * owners : (j + 1) * owners]
    for at in range(total_slots):
        if at not in used:
            ens_stage[:, at, :] = jnp.zeros((owners, cols), F32)
    snd_e[...] = ens_stage[...].astype(BF16)
    enses.start()

    for load in loads[8:]:
        load.wait()

    def filtered(xs):
        pieces = xs
        spectra = [real_dft(piece) for piece in pieces]
        res, ims = [], []
        for k1 in range(residues):
            parts_re, parts_im = [], []
            for h in range(halves):
                c = tw_c[k1 : k1 + 1, h * LANES : (h + 1) * LANES]
                s = tw_s[k1 : k1 + 1, h * LANES : (h + 1) * LANES]
                re, im = spectra[h][k1]
                if k1 == 0:
                    parts_re.append(re)
                    parts_im.append(jnp.zeros_like(re))
                elif im is None:
                    parts_re.append(re * c)
                    parts_im.append(-re * s)
                else:
                    parts_re.append(re * c + im * s)
                    parts_im.append(im * c - re * s)
            res.append(jnp.concatenate(parts_re + parts_im, axis=1))
        y_hi, y_lo = split2(jnp.concatenate(res, axis=0))
        z = dot(y_hi, fwd_hi[...]) + dot(y_lo, fwd_hi[...]) + dot(y_hi, fwd_lo[...])
        z = jnp.concatenate(
            [z[k1 * slots : (k1 + 1) * slots] * waves[k1 : k1 + 1, :] for k1 in range(residues)], axis=0
        )
        z_hi, z_lo = split2(z)
        v = dot(z_hi, inv_hi[...]) + dot(z_lo, inv_hi[...]) + dot(z_hi, inv_lo[...])
        outs = []
        for h in range(halves):
            zs = []
            for k1 in range(residues):
                c = tw_c[k1 : k1 + 1, h * LANES : (h + 1) * LANES]
                s = tw_s[k1 : k1 + 1, h * LANES : (h + 1) * LANES]
                at = slice(k1 * slots, (k1 + 1) * slots)
                re = v[at, h * LANES : (h + 1) * LANES]
                im = v[at, cols + h * LANES : cols + (h + 1) * LANES]
                zs.append((re, im) if k1 == 0 else (re * c - im * s, im * c + re * s))
            outs.append(real_sum(zs, parts))
        return outs

    at_slot = lax.broadcasted_iota(jnp.int32, (slots, cols), 0)

    def inc_copy(i, j):
        return pltpu.make_async_remote_copy(
            src_ref=snd_i.at[i], dst_ref=rcv_i.at[group, mine],
            send_sem=i_send.at[i, j], recv_sem=i_recv.at[group, mine],
            device_id={"grp": lax.rem(group + j, groups), "sp": lax.rem(part + parts - i, parts)},
        )

    def out_copy(i):
        to = lax.rem(part + i, parts)
        return pltpu.make_async_remote_copy(
            src_ref=snd_o.at[to], dst_ref=rcv_o.at[mine],
            send_sem=o_send.at[i], recv_sem=o_recv.at[mine], device_id={"sp": to},
        )

    @pl.when(owner)
    def _():
        count = spectrum.shape[1]
        inner = count // parts
        wave = lax.broadcasted_iota(jnp.int32, (waves.shape[0], count), 1)
        residue = lax.broadcasted_iota(jnp.int32, wave.shape, 0)
        weights = jnp.broadcast_to(spectrum[...], wave.shape)
        forward = jnp.where((lax.rem(wave, parts) == residue) & (residue < residues), weights, 0.0)
        mirrored = (lax.rem(wave + residue, parts) == 0) & (residue > 0) & (residue < residues - 1)
        backward = jnp.where(mirrored, weights, 0.0)
        k = lax.broadcasted_iota(jnp.int32, (count, 4 * inner), 0)
        j = lax.rem(lax.broadcasted_iota(jnp.int32, (count, 4 * inner), 1), 2 * inner)
        ahead, behind = k - parts * (j - inner), k - parts * (inner - 1 - j)
        ahead = jnp.where((ahead >= 0) & (ahead < parts), 1.0, 0.0).astype(BF16)
        behind = jnp.where((behind >= 0) & (behind < parts), 1.0, 0.0).astype(BF16)
        f_hi, f_lo = split2(forward)
        b_hi, b_lo = split2(backward)
        waves[...] = dot(f_hi, ahead) + dot(f_lo, ahead) + dot(b_hi, behind) + dot(b_lo, behind)

        alphas.take_own()
        enses.take_own()
        for i in range(1, parts):
            alphas.receive(i)
        came = [[None] * parts for _ in range(halves)]
        for p in range(parts):
            x = rcv_a[p].astype(F32)
            for h in range(halves):
                came[h][p] = (x if h == 0 else pltpu.roll(x, x.shape[0] - h * items, 0))[:slots]
        localized = filtered(came)
        for p in range(parts):
            loc = jnp.concatenate([localized[h][p] for h in range(halves)], axis=1)
            loc_buf[p] = loc.astype(BF16).astype(F32)
        lane = lax.broadcasted_iota(jnp.int32, (8, LANES), 1)
        at_row = lax.broadcasted_iota(jnp.int32, (8, LANES), 0)
        tiles = [None] * parts

        def increments(p):
            loc = loc_buf[p]
            a = rcv_e[p, :slots].astype(F32) * jnp.where(at_slot < items, loc, pltpu.roll(loc, items, 0))
            b = rcv_e[p, slots : 2 * slots].astype(F32) * jnp.where(at_slot < items, loc, pltpu.roll(loc, items - spare, 0))
            rest = total_slots - 2 * slots
            c = rcv_e[p, 2 * slots :].astype(F32) * loc[2 * spare : 2 * spare + rest]
            hi, lo = split2(jnp.concatenate([a, b, c], axis=0))
            return spread * dot(pick[...], jnp.concatenate([hi, lo], axis=0))

        def put_increments(i):
            after, before = tiles[i - 1][:, :LANES], tiles[(i + 1) % parts][:, cols - LANES :]
            ends = jnp.where(lane < LANES // 2, after, before)
            pieces = [tiles[i][:, h * LANES : (h + 1) * LANES] for h in range(halves)]
            for v in range(3):
                window = (lane >= 2 * HALO * v) & (lane < 2 * HALO * (v + 1)) & (at_row >= 3 * per)
                moved = pltpu.roll(ends, 2 * HALO * v + HALO, 1)
                if 3 * per - per * v:
                    moved = pltpu.roll(moved, 3 * per - per * v, 0)
                pieces[0] = jnp.where(window, moved, pieces[0])
            snd_i[i] = jnp.concatenate(pieces, axis=0).astype(BF16)

        pl.semaphore_wait(whole, groups - 1)
        batch = owners // BATCHES
        for first_of in range(0, owners, batch):
            blocks = [i for k in range(first_of, first_of + batch) for i in (k, k + owners)]
            for i in blocks:
                if i > 0:
                    enses.receive(i)
            for i in blocks:
                tiles[i] = increments(lax.rem(part + parts - i, parts))
            ready = [i for k in range(first_of - 1, first_of + batch - 1) if k > 0 for i in (k, k + owners)]
            if first_of + batch == owners:
                ready += [owners - 1, parts - 1, 0, owners]
            for i in ready:
                put_increments(i)
            for i in ready:
                for j in range(groups):
                    if i + j > 0:
                        inc_copy(i, j).start()
        rcv_i[group, mine] = snd_i[0]

    for copy in field_copies:
        copy.wait_recv()
    lane = lax.broadcasted_iota(jnp.int32, (tile_rows, LANES), 1)
    for g in range(groups):
        at = slice(g * tile_rows, (g + 1) * tile_rows)
        for f in range(9):
            wide[f, at, :cols] = rcv_f[g, f]
            if f in haloed:
                back = LANES - (2 * HALO * haloed.index(f) + HALO)
                before, after = (pltpu.roll(rcv_edge[side, g], back, 1) for side in (0, 1))
                wide[f, at, cols:] = jnp.where(lane < LANES // 2, after, before)
            else:
                wide[f, at, cols:] = jnp.zeros((tile_rows, LANES), F32)

    for j in range(groups):
        for k in range(owners):
            g, at = lax.rem(group + j, groups), lax.rem(part + k, owners)
            arrival = pltpu.make_async_remote_copy(
                src_ref=snd_i.at[0], dst_ref=rcv_i.at[g, at],
                send_sem=i_send.at[0, 0], recv_sem=i_recv.at[g, at], device_id={"sp": left},
            )
            if j == 0:
                pl.when(at != mine)(arrival.wait_recv)
            else:
                arrival.wait_recv()
    total = rcv_i[0].astype(F32)
    for g in range(1, groups):
        total = total + rcv_i[g].astype(F32)
    message[...] = total

    def gathered(index):
        return jnp.concatenate([message[:, index + j, :] for j in range(per)], axis=0)

    ends = gathered(3 * per)
    state0 = []
    for v in range(3):
        pieces = [gathered(8 * h + per * v) for h in range(halves)]
        pieces.append(pltpu.roll(ends, LANES - (2 * HALO * v + HALO), 1))
        state0.append(jnp.concatenate(pieces, axis=1) + wide[v])
    row_at = lax.broadcasted_iota(jnp.int32, (rows, cols + LANES), 0).astype(F32)
    rotation = 0.1 + 0.2 * (row_at + 0.5) / rows
    state1 = model_step(state0, rotation)
    state2 = model_step(state1, rotation)
    forcing = [wide[3 + t] * s[0] - wide[6 + t] for t, s in enumerate((state0, state1, state2))]
    zero = jnp.zeros_like(rotation)
    h, u, w = adjoint_step((forcing[2], zero, zero), rotation)
    h, u, w = adjoint_step((h + forcing[1], u, w), rotation)
    for v, field in enumerate((h + forcing[0], u, w)):
        field = field[:, :cols]
        adjoint[v] = field
        half = field.astype(BF16).astype(F32)
        for h in range(halves):
            for j in range(per):
                message[:, 8 * h + per * v + j, :] = half[j * owners : (j + 1) * owners, h * LANES : (h + 1) * LANES]
    snd_h[...] = message[...].astype(BF16)
    halfs.start()
    for v in range(3):
        grad_control_ref[v] = control[v] + std[v] * adjoint[v, tile, :]

    @pl.when(owner)
    def _():
        halfs.take_own()
        for i in range(1, parts):
            halfs.receive(i)
        weighted = []
        for p in range(parts):
            came_h = rcv_h[p].astype(F32)

            def row_of(v, j):
                pieces = [came_h[8 * h + per * v + j : 8 * h + per * v + j + 1] for h in range(halves)]
                return jnp.broadcast_to(jnp.concatenate(pieces, axis=1), (slots, cols))

            def field_of(v, count):
                out = row_of(v, per - 1)
                for j in reversed(range(per - 1)):
                    out = jnp.where(at_slot < (j + 1) * members, row_of(v, j), out)
                return out

            third = field_of(2, items)
            a = rcv_e[p, :slots].astype(F32) * jnp.where(at_slot < items, field_of(0, items), pltpu.roll(third, items, 0))
            b = rcv_e[p, slots : 2 * slots].astype(F32) * jnp.where(
                at_slot < items, field_of(1, items), pltpu.roll(third, items - spare, 0)
            )
            rest = total_slots - 2 * slots
            c = rcv_e[p, 2 * slots :].astype(F32) * third[2 * spare : 2 * spare + rest]
            own = jnp.concatenate([jnp.zeros((2 * spare, cols), F32), c], axis=0)[:slots]
            own = jnp.where(at_slot < 2 * spare, pltpu.roll(b, slots - (items - spare), 0), own)
            own = jnp.where(at_slot < spare, pltpu.roll(a, slots - items, 0), own)
            weighted.append(a + b + own)
        outs = filtered([[x[:, h * LANES : (h + 1) * LANES] for x in weighted] for h in range(halves)])
        for p in range(parts):
            for h in range(halves):
                out_stage[p, h * items : (h + 1) * items, :] = outs[h][p][:items]
            snd_o[p] = out_stage[p].astype(BF16)
        for i in range(1, parts):
            out_copy(i).start()
        rcv_o[mine] = snd_o[part]

    for k in range(owners):
        at = lax.rem(part + k, owners)
        arrival = pltpu.make_async_remote_copy(
            src_ref=snd_o.at[0], dst_ref=rcv_o.at[at],
            send_sem=o_send.at[0], recv_sem=o_recv.at[at], device_id={"sp": left},
        )
        pl.when(at != mine)(arrival.wait_recv)
    stage[...] = rcv_o[...].astype(F32)
    for m in range(members):
        for j in range(per):
            for h in range(halves):
                at, lanes = slice(j * owners, (j + 1) * owners), slice(h * LANES, (h + 1) * LANES)
                corr_ref[m, at, lanes] = alpha[m, at, lanes] + spread * stage[:, h * items + j * members + m, :]
    alphas.finish()
    enses.finish()
    halfs.finish()
    for copy in field_copies:
        copy.wait_send()

    @pl.when(owner)
    def _():
        for i in range(parts):
            for j in range(groups):
                if i + j > 0:
                    inc_copy(i, j).wait_send()
        for i in range(1, parts):
            out_copy(i).wait_send()


def finish(corr_ref, grad_control_ref, corr_out, grad_control_out, sem):
    copies = [
        pltpu.make_async_copy(corr_ref, corr_out, sem.at[0]),
        pltpu.make_async_copy(grad_control_ref, grad_control_out, sem.at[1]),
    ]
    for copy in copies:
        copy.start()
    for copy in copies:
        copy.wait()


def tables(parts, cols, waves, members, rows):
    length = parts * cols
    inner = waves // parts
    residues = parts // 2 + 1
    twist = 2 * np.pi * np.outer(np.arange(residues), np.arange(cols)) / length
    quotient = np.arange(-inner, inner)
    phase = 2 * np.pi * (np.outer(np.arange(cols), quotient) % cols) / cols
    c, s = np.cos(phase), np.sin(phase)
    forward = np.block([[c, -s], [s, c]])
    owners, per, items, slots, spare, total_slots = layout(members, rows, parts)
    pick = np.zeros((8, 2, total_slots), np.float32)
    for v in range(3):
        for j in range(per):
            for m in range(members):
                pick[v * per + j, :, slot_of(v, j * members + m, items, slots, spare)] = 1.0
    return (
        *both(forward), *both(forward.T.copy()), np.cos(twist).astype(np.float32), np.sin(twist).astype(np.float32),
        pick.reshape(8, 2 * total_slots).astype(BF16),
    )


def per_device(alpha, ensemble, static_std, control, loc_spectrum, obs_cell, obs_step, innovation, obs_weight):
    members, rows, cols = alpha.shape
    groups, parts = lax.axis_size("grp"), lax.axis_size("sp")
    spread = 1.0 / math.sqrt(members * groups - 1)
    owners, per, items, slots, spare, total_slots = layout(members, rows, parts)
    assert owners * per == rows and 4 * per <= 8 and spare % 4 == 0
    tile_rows = control.shape[1]
    halves = cols // LANES
    residues = parts // 2 + 1
    inner = loc_spectrum.shape[0] // parts
    operands = (
        alpha, ensemble, static_std, control, loc_spectrum[None],
        obs_cell[None], obs_step[None], innovation[None], obs_weight[None],
        *tables(parts, cols, loc_spectrum.shape[0], members, rows),
    )
    packed = (round8(halves * items), LANES)
    message = (8 * halves, LANES)
    vmem = pl.BlockSpec(memory_space=pltpu.VMEM)
    dma = pltpu.SemaphoreType.DMA
    corr, grad_control = pl.pallas_call(
        functools.partial(kernel, groups, parts, spread),
        out_shape=(
            pltpu.VMEM(alpha.shape, F32),
            pltpu.VMEM(control.shape, F32),
        ),
        in_specs=[HBM] * len(operands),
        out_specs=(vmem, vmem),
        scratch_shapes=[
            *[pltpu.VMEM(t.shape, t.dtype) for t in operands],
            pltpu.VMEM((owners, *packed), F32),
            pltpu.VMEM((parts, *packed), F32),
            pltpu.VMEM((owners, total_slots, cols), F32),
            pltpu.VMEM((parts, slots, cols), F32),
            pltpu.VMEM((3, rows, cols), F32),
            pltpu.VMEM((round8(residues), 4 * inner), F32),
            pltpu.VMEM((9, tile_rows, cols), F32),
            pltpu.VMEM((9, rows, cols + LANES), F32),
            pltpu.VMEM((owners, *message), F32),
            pltpu.VMEM((owners, *packed), BF16), pltpu.VMEM((parts, *packed), BF16),
            pltpu.VMEM((owners, total_slots, cols), BF16), pltpu.VMEM((parts, total_slots, cols), BF16),
            pltpu.VMEM((parts, *message), BF16), pltpu.VMEM((groups, owners, *message), BF16),
            pltpu.VMEM((owners, *message), BF16), pltpu.VMEM((parts, *message), BF16),
            pltpu.VMEM((parts, *packed), BF16), pltpu.VMEM((owners, *packed), BF16),
            pltpu.VMEM((groups, 9, tile_rows, cols), F32),
            pltpu.VMEM((tile_rows, LANES), F32), pltpu.VMEM((2, groups, tile_rows, LANES), F32),
            dma((len(operands),)),
            dma((owners,)), dma((parts,)), dma((owners,)), dma((parts,)),
            dma((parts, groups)), dma((groups, owners)),
            dma((owners,)), dma((parts,)), dma((parts,)), dma((owners,)),
            dma((3, groups)), dma((3, groups)),
            pltpu.SemaphoreType.REGULAR,
        ],
        compiler_params=pltpu.CompilerParams(collective_id=0, has_side_effects=True, vmem_limit_bytes=63 << 20),
    )(*operands)
    return pl.pallas_call(
        finish,
        out_shape=(jax.ShapeDtypeStruct(alpha.shape, F32), jax.ShapeDtypeStruct(control.shape, F32)),
        in_specs=[vmem] * 2,
        out_specs=(HBM, HBM),
        scratch_shapes=[dma((2,))],
        compiler_params=pltpu.CompilerParams(vmem_limit_bytes=1 << 20),
    )(corr, grad_control)


def solution(mesh):
    flat = P(("grp", "sp"))
    tile = P(None, "grp", "sp")
    return jax.shard_map(
        per_device,
        mesh=mesh,
        in_specs=(P("grp", None, "sp"), P("grp", None, None, "sp"), tile, tile, P(), flat, flat, flat, flat),
        out_specs=(P("grp", None, "sp"), tile),
        check_vma=False,
    )
```

time: 35 us -> 32.9 us (0.940)
  Pallas kernels: 34.3 us -> 32.1 us
    pallas_call x1, Pallas kernels: 33.6 us -> 31.4 us  [per_device(): pl.pallas_call(functools.partial(kernel, groups, parts, spread), out_shap...]
where the time goes in v4:
time: 32.9 us; the launch traced here: 32.7 us
  Pallas kernels  32.1 us (98%)
  between operations  0.64 us (2%)
    pallas_call x1, Pallas kernels, per_device(): pl.pallas_call(functools.partial(kernel, groups, parts, spread), out_shap...  31.4 us
    pallas_call x1, Pallas kernels, per_device(): pl.pallas_call(finish, out_shape=(jax.ShapeDtypeStruct(alpha.shape, F32),...  0.69 us

profile of v4, /device:TPU:0, one launch (start us, length us, event | category | flops | bytes accessed | tf_op | source)
XLA Modules:
  0.0 32.7 jit_solution(5503013034050805665)
XLA Ops:
  0.6 31.4 %shard_map.167 = (f32[10,16,256]{2,1,0:T(8,128)S(1)}, f32[3,8,256]{2,1,0:T(8,128)S(1)}) custom-call(f32[10,16,256]{2,1,0:T(8,128)} %alpha_any.1, bf16[10,3,16,256]{3,2,1,0:T(8,128)(2,1)} %ens_any.1, f32[3,8,256]{2,1,0:T(8,128)} %std_any.1, f32[3,8,256]{2,1,0:T(8,128)} %control_any.1, f32[1,1024]{1,0:T(1,128)} %bitcast.5, s32[1,1024]{1,0:T(1,128)} %bitcast.6, ...), custom_call_target="tpu_custom_call" | custom-call | tf_op jit(solution)/shard_map/pallas_call | solution.py:630
  32.0 0.7 %shard_map.168 = (f32[10,16,256]{2,1,0:T(8,128)}, f32[3,8,256]{2,1,0:T(8,128)}) custom-call(f32[10,16,256]{2,1,0:T(8,128)S(1)} %get-tuple-element.4.corr_ref, f32[3,8,256]{2,1,0:T(8,128)S(1)} %get-tuple-element.5.grad_control_ref), custom_call_target="tpu_custom_call" | custom-call | tf_op jit(solution)/shard_map/pallas_call | solution.py:665

commit v5 on v4

--- a/solution.py
+++ b/solution.py
@@ -153,7 +153,7 @@
     fwd_hi, fwd_lo, inv_hi, inv_lo, tw_c, tw_s, pick,
     stage, out_stage, ens_stage, loc_buf, adjoint, waves, fields, wide, message,
     snd_a, rcv_a, snd_e, rcv_e, snd_i, rcv_i, snd_h, rcv_h, snd_o, rcv_o, rcv_f, edge, rcv_edge,
-    load_sem, a_send, a_recv, e_send, e_recv, i_send, i_recv, h_send, h_recv, o_send, o_recv, f_send, f_recv, whole,
+    load_sem, a_send, a_recv, e_send, e_recv, i_send, i_recv, h_send, h_recv, o_send, o_recv, f_send, f_recv, here, whole, go,
 ):
     group, part = lax.axis_index("grp"), lax.axis_index("sp")
     left, right = lax.rem(part + parts - 1, parts), lax.rem(part + 1, parts)
@@ -168,20 +168,14 @@
     residues = parts // 2 + 1
 
     barrier = pltpu.get_barrier_semaphore()
-    others = [(0, left), (0, right)] + [(j, at) for j in range(1, groups) for at in (part, left, right)]
 
     @pl.when(owner)
     def _():
         for i in range(1, parts):
             pl.semaphore_signal(barrier, inc=1, device_id={"sp": lax.rem(part + i, parts)})
 
-    @pl.when(jnp.logical_not(owner))
-    def _():
-        for i in range(owners):
-            pl.semaphore_signal(barrier, inc=1, device_id={"sp": low + lax.rem(part + i, owners)})
-
-    for j, at in others:
-        pl.semaphore_signal(barrier, inc=1, device_id={"grp": lax.rem(group + j, groups), "sp": at})
+    for j in range(1, groups):
+        pl.semaphore_signal(barrier, inc=1, device_id={"grp": lax.rem(group + j, groups)})
 
     pairs = [
         (alpha_any, alpha), (ens_any, ens), (cell_any, cell), (step_any, step), (innovation_any, innovation),
@@ -204,6 +198,66 @@
                     alpha[m, j * owners : (j + 1) * owners, h * LANES : (h + 1) * LANES]
                 )
     snd_a[...] = stage[...].astype(BF16)
+
+    @pl.when(owner)
+    def _():
+        pl.semaphore_wait(barrier, owners + groups - 2)
+
+    @pl.when(jnp.logical_not(owner))
+    def _():
+        pl.semaphore_wait(barrier, owners + groups - 1)
+        for i in range(owners):
+            pl.semaphore_signal(here, inc=1, device_id={"sp": low + lax.rem(part + i, owners)})
+
+    class ToOwners:
+        def __init__(self, source, target, send, recv):
+            self.source, self.target, self.send, self.recv = source, target, send, recv
+
+        def copy(self, i):
+            at = lax.rem(part + i, owners)
+            return low + at, pltpu.make_async_remote_copy(
+                src_ref=self.source.at[at], dst_ref=self.target.at[part],
+                send_sem=self.send.at[i], recv_sem=self.recv.at[part], device_id={"sp": low + at},
+            )
+
+        def start(self):
+            for i in range(owners):
+                to, copy = self.copy(i)
+                pl.when(to != part)(copy.start)
+
+        def take_own(self):
+            self.target[part] = self.source[mine]
+
+        def receive(self, i):
+            at = lax.rem(part + parts - i, parts)
+            pltpu.make_async_remote_copy(
+                src_ref=self.source.at[0], dst_ref=self.target.at[at],
+                send_sem=self.send.at[0], recv_sem=self.recv.at[at], device_id={"sp": left},
+            ).wait_recv()
+
+        def finish(self):
+            for i in range(owners):
+                to, copy = self.copy(i)
+                pl.when(to != part)(copy.wait_send)
+
+    alphas = ToOwners(snd_a, rcv_a, a_send, a_recv)
+    enses = ToOwners(snd_e, rcv_e, e_send, e_recv)
+    halfs = ToOwners(snd_h, rcv_h, h_send, h_recv)
+    alphas.start()
+    loads[1].wait()
+    used = set()
+    for v in range(3):
+        for m in range(members):
+            field = ens[m, v].astype(F32)
+            for j in range(per):
+                at = slot_of(v, j * members + m, items, slots, spare)
+                used.add(at)
+                ens_stage[:, at, :] = field[j * owners : (j + 1) * owners]
+    for at in range(total_slots):
+        if at not in used:
+            ens_stage[:, at, :] = jnp.zeros((owners, cols), F32)
+    snd_e[...] = ens_stage[...].astype(BF16)
+    enses.start()
 
     for load in loads[2:8]:
         load.wait()
@@ -238,85 +292,27 @@
         packed = jnp.where(window, pltpu.roll(ends, (2 * HALO * e + HALO) % LANES, 1), packed)
     edge[...] = packed
 
+    rcv_f[group] = fields[...]
+    full_copies = [
+        pltpu.make_async_remote_copy(
+            src_ref=fields, dst_ref=rcv_f.at[group],
+            send_sem=f_send.at[0, j], recv_sem=f_recv.at[0, j], device_id={"grp": lax.rem(group + j, groups)},
+        )
+        for j in range(1, groups)
+    ]
+    for copy in full_copies:
+        copy.start()
+
     @pl.when(owner)
     def _():
-        pl.semaphore_wait(barrier, parts - 1 + len(others))
+        pl.semaphore_wait(here, parts - owners)
         for j in range(1, groups):
             pl.semaphore_signal(whole, inc=1, device_id={"grp": lax.rem(group + j, groups)})
 
-    @pl.when(jnp.logical_not(owner))
-    def _():
-        pl.semaphore_wait(barrier, owners + len(others))
-
-    class ToOwners:
-        def __init__(self, source, target, send, recv):
-            self.source, self.target, self.send, self.recv = source, target, send, recv
-
-        def copy(self, i):
-            at = lax.rem(part + i, owners)
-            return low + at, pltpu.make_async_remote_copy(
-                src_ref=self.source.at[at], dst_ref=self.target.at[part],
-                send_sem=self.send.at[i], recv_sem=self.recv.at[part], device_id={"sp": low + at},
-            )
-
-        def start(self):
-            for i in range(owners):
-                to, copy = self.copy(i)
-                pl.when(to != part)(copy.start)
-
-        def take_own(self):
-            self.target[part] = self.source[mine]
-
-        def receive(self, i):
-            at = lax.rem(part + parts - i, parts)
-            pltpu.make_async_remote_copy(
-                src_ref=self.source.at[0], dst_ref=self.target.at[at],
-                send_sem=self.send.at[0], recv_sem=self.recv.at[at], device_id={"sp": left},
-            ).wait_recv()
-
-        def finish(self):
-            for i in range(owners):
-                to, copy = self.copy(i)
-                pl.when(to != part)(copy.wait_send)
-
-    alphas = ToOwners(snd_a, rcv_a, a_send, a_recv)
-    enses = ToOwners(snd_e, rcv_e, e_send, e_recv)
-    halfs = ToOwners(snd_h, rcv_h, h_send, h_recv)
-    alphas.start()
-    field_copies = []
-    for j in range(groups):
-        to = lax.rem(group + j, groups)
-        plans = [(1, right, edge, rcv_edge.at[0, group]), (2, left, edge, rcv_edge.at[1, group])]
-        if j > 0:
-            plans.append((0, part, fields, rcv_f.at[group]))
-        for kind, at, source, target in plans:
-            field_copies.append(pltpu.make_async_remote_copy(
-                src_ref=source, dst_ref=target,
-                send_sem=f_send.at[kind, j], recv_sem=f_recv.at[kind, j], device_id={"grp": to, "sp": at},
-            ))
-            field_copies[-1].start()
-    rcv_f[group] = fields[...]
-
-
-    loads[1].wait()
-    used = set()
-    for v in range(3):
-        for m in range(members):
-            field = ens[m, v].astype(F32)
-            for j in range(per):
-                at = slot_of(v, j * members + m, items, slots, spare)
-                used.add(at)
-                ens_stage[:, at, :] = field[j * owners : (j + 1) * owners]
-    for at in range(total_slots):
-        if at not in used:
-            ens_stage[:, at, :] = jnp.zeros((owners, cols), F32)
-    snd_e[...] = ens_stage[...].astype(BF16)
-    enses.start()
-
     for load in loads[8:]:
         load.wait()
 
-    def filtered(xs):
+    def filtered(xs, exact):
         pieces = xs
         spectra = [real_dft(piece) for piece in pieces]
         res, ims = [], []
@@ -337,12 +333,16 @@
                     parts_im.append(im * c - re * s)
             res.append(jnp.concatenate(parts_re + parts_im, axis=1))
         y_hi, y_lo = split2(jnp.concatenate(res, axis=0))
-        z = dot(y_hi, fwd_hi[...]) + dot(y_lo, fwd_hi[...]) + dot(y_hi, fwd_lo[...])
+        z = dot(y_hi, fwd_hi[...])
+        if exact:
+            z = z + dot(y_lo, fwd_hi[...]) + dot(y_hi, fwd_lo[...])
         z = jnp.concatenate(
             [z[k1 * slots : (k1 + 1) * slots] * waves[k1 : k1 + 1, :] for k1 in range(residues)], axis=0
         )
         z_hi, z_lo = split2(z)
-        v = dot(z_hi, inv_hi[...]) + dot(z_lo, inv_hi[...]) + dot(z_hi, inv_lo[...])
+        v = dot(z_hi, inv_hi[...])
+        if exact:
+            v = v + dot(z_lo, inv_hi[...]) + dot(z_hi, inv_lo[...])
         outs = []
         for h in range(halves):
             zs = []
@@ -366,7 +366,7 @@
         )
 
     def out_copy(i):
-        to = lax.rem(part + i, parts)
+        to = i
         return pltpu.make_async_remote_copy(
             src_ref=snd_o.at[to], dst_ref=rcv_o.at[mine],
             send_sem=o_send.at[i], recv_sem=o_recv.at[mine], device_id={"sp": to},
@@ -400,10 +400,37 @@
             x = rcv_a[p].astype(F32)
             for h in range(halves):
                 came[h][p] = (x if h == 0 else pltpu.roll(x, x.shape[0] - h * items, 0))[:slots]
-        localized = filtered(came)
+        localized = filtered(came, True)
         for p in range(parts):
             loc = jnp.concatenate([localized[h][p] for h in range(halves)], axis=1)
             loc_buf[p] = loc.astype(BF16).astype(F32)
+    @pl.when(owner)
+    def _():
+        if groups > 1:
+            pl.semaphore_wait(whole, groups - 1)
+        for i in range(parts // owners):
+            to = mine * (parts // owners) + i
+
+            @pl.when(to != part)
+            def _():
+                pl.semaphore_signal(go, inc=1, device_id={"sp": to})
+
+    @pl.when(part // (parts // owners) != mine)
+    def _():
+        pl.semaphore_wait(go, 1)
+
+    end_copies = []
+    for j in range(groups):
+        for kind, at, target in ((1, right, rcv_edge.at[0, group]), (2, left, rcv_edge.at[1, group])):
+            end_copies.append(pltpu.make_async_remote_copy(
+                src_ref=edge, dst_ref=target, send_sem=f_send.at[kind, j], recv_sem=f_recv.at[kind, j],
+                device_id={"grp": lax.rem(group + j, groups), "sp": at},
+            ))
+            end_copies[-1].start()
+    field_copies = full_copies + end_copies
+
+    @pl.when(owner)
+    def _():
         lane = lax.broadcasted_iota(jnp.int32, (8, LANES), 1)
         at_row = lax.broadcasted_iota(jnp.int32, (8, LANES), 0)
         tiles = [None] * parts
@@ -429,7 +456,6 @@
                 pieces[0] = jnp.where(window, moved, pieces[0])
             snd_i[i] = jnp.concatenate(pieces, axis=0).astype(BF16)
 
-        pl.semaphore_wait(whole, groups - 1)
         batch = owners // BATCHES
         for first_of in range(0, owners, batch):
             blocks = [i for k in range(first_of, first_of + batch) for i in (k, k + owners)]
@@ -538,13 +564,13 @@
             own = jnp.where(at_slot < 2 * spare, pltpu.roll(b, slots - (items - spare), 0), own)
             own = jnp.where(at_slot < spare, pltpu.roll(a, slots - items, 0), own)
             weighted.append(a + b + own)
-        outs = filtered([[x[:, h * LANES : (h + 1) * LANES] for x in weighted] for h in range(halves)])
+        outs = filtered([[x[:, h * LANES : (h + 1) * LANES] for x in weighted] for h in range(halves)], False)
         for p in range(parts):
             for h in range(halves):
                 out_stage[p, h * items : (h + 1) * items, :] = outs[h][p][:items]
             snd_o[p] = out_stage[p].astype(BF16)
-        for i in range(1, parts):
-            out_copy(i).start()
+        for i in range(parts):
+            pl.when(part != i)(out_copy(i).start)
         rcv_o[mine] = snd_o[part]
 
     for k in range(owners):
@@ -572,8 +598,8 @@
             for j in range(groups):
                 if i + j > 0:
                     inc_copy(i, j).wait_send()
-        for i in range(1, parts):
-            out_copy(i).wait_send()
+        for i in range(parts):
+            pl.when(part != i)(out_copy(i).wait_send)
 
 
 def finish(corr_ref, grad_control_ref, corr_out, grad_control_out, sem):
@@ -658,7 +684,7 @@
             dma((parts, groups)), dma((groups, owners)),
             dma((owners,)), dma((parts,)), dma((parts,)), dma((owners,)),
             dma((3, groups)), dma((3, groups)),
-            pltpu.SemaphoreType.REGULAR,
+            pltpu.SemaphoreType.REGULAR, pltpu.SemaphoreType.REGULAR, pltpu.SemaphoreType.REGULAR,
         ],
         compiler_params=pltpu.CompilerParams(collective_id=0, has_side_effects=True, vmem_limit_bytes=63 << 20),
     )(*operands)

time: 32.9 us -> 32.2 us (0.979)
  Pallas kernels: 32.1 us -> 31.4 us
    pallas_call x1, Pallas kernels: 31.4 us -> 30.7 us  [per_device(): pl.pallas_call(functools.partial(kernel, groups, parts, spread), out_shap...]
where the time goes in v5:
time: 32.2 us; the launch traced here: 32 us
  Pallas kernels  31.4 us (98%)
  between operations  0.64 us (2%)
    pallas_call x1, Pallas kernels, per_device(): pl.pallas_call(functools.partial(kernel, groups, parts, spread), out_shap...  30.7 us
    pallas_call x1, Pallas kernels, per_device(): pl.pallas_call(finish, out_shape=(jax.ShapeDtypeStruct(alpha.shape, F32),...  0.69 us

profile of v5, /device:TPU:0, one launch (start us, length us, event | category | flops | bytes accessed | tf_op | source)
XLA Modules:
  0.0 32.0 jit_solution(8839065782412432065)
XLA Ops:
  0.6 30.7 %shard_map.167 = (f32[10,16,256]{2,1,0:T(8,128)S(1)}, f32[3,8,256]{2,1,0:T(8,128)S(1)}) custom-call(f32[10,16,256]{2,1,0:T(8,128)} %alpha_any.1, bf16[10,3,16,256]{3,2,1,0:T(8,128)(2,1)} %ens_any.1, f32[3,8,256]{2,1,0:T(8,128)} %std_any.1, f32[3,8,256]{2,1,0:T(8,128)} %control_any.1, f32[1,1024]{1,0:T(1,128)} %bitcast.5, s32[1,1024]{1,0:T(1,128)} %bitcast.6, ...), custom_call_target="tpu_custom_call" | custom-call | tf_op jit(solution)/shard_map/pallas_call | solution.py:656
  31.3 0.7 %shard_map.168 = (f32[10,16,256]{2,1,0:T(8,128)}, f32[3,8,256]{2,1,0:T(8,128)}) custom-call(f32[10,16,256]{2,1,0:T(8,128)S(1)} %get-tuple-element.4.corr_ref, f32[3,8,256]{2,1,0:T(8,128)S(1)} %get-tuple-element.5.grad_control_ref), custom_call_target="tpu_custom_call" | custom-call | tf_op jit(solution)/shard_map/pallas_call | solution.py:691

commit v6 on v5

--- a/solution.py
+++ b/solution.py
@@ -134,6 +134,13 @@
     return owners, per, items, slots, spare, 2 * slots + round8(items - 2 * spare)
 
 
+def half_row(slot, half, halves, used):
+    whole_rows = used // 8 * 8
+    if slot < whole_rows:
+        return half * whole_rows + slot
+    return halves * whole_rows + half * (used - whole_rows) + slot - whole_rows
+
+
 def slot_of(v, item, items, slots, spare):
     if v < 2:
         return v * slots + item
@@ -161,6 +168,7 @@
     tile_rows = control.shape[1]
     tile = pl.ds(pl.multiple_of(group * tile_rows, tile_rows), tile_rows)
     owners, per, items, slots, spare, total_slots = layout(members, rows, parts)
+    used = 3 * items
     low = parts // 4
     mine = part - low
     owner = (part >= low) & (part < low + owners)
@@ -245,17 +253,15 @@
     halfs = ToOwners(snd_h, rcv_h, h_send, h_recv)
     alphas.start()
     loads[1].wait()
-    used = set()
+    if ens_stage.shape[1] > halves * used:
+        ens_stage[:, halves * used :, :] = jnp.zeros((owners, ens_stage.shape[1] - halves * used, LANES), F32)
     for v in range(3):
         for m in range(members):
             field = ens[m, v].astype(F32)
             for j in range(per):
-                at = slot_of(v, j * members + m, items, slots, spare)
-                used.add(at)
-                ens_stage[:, at, :] = field[j * owners : (j + 1) * owners]
-    for at in range(total_slots):
-        if at not in used:
-            ens_stage[:, at, :] = jnp.zeros((owners, cols), F32)
+                for h in range(halves):
+                    at = half_row(slot_of(v, j * members + m, items, slots, spare), h, halves, used)
+                    ens_stage[:, at, :] = field[j * owners : (j + 1) * owners, h * LANES : (h + 1) * LANES]
     snd_e[...] = ens_stage[...].astype(BF16)
     enses.start()
 
@@ -358,6 +364,17 @@
 
     at_slot = lax.broadcasted_iota(jnp.int32, (slots, cols), 0)
 
+    def ens_rows(p, first_slot, last_slot):
+        full = used // 8 * 8
+        pieces = []
+        for h in range(halves):
+            rows_of = [rcv_e[p, h * full + first_slot : h * full + min(last_slot, full)].astype(F32)]
+            if last_slot > full:
+                tail = rcv_e[p, halves * full : halves * full + 8].astype(F32)
+                rows_of.append(tail if h == 0 else pltpu.roll(tail, 8 - h * (used - full), 0))
+            pieces.append(jnp.concatenate(rows_of, axis=0))
+        return jnp.concatenate(pieces, axis=1)
+
     def inc_copy(i, j):
         return pltpu.make_async_remote_copy(
             src_ref=snd_i.at[i], dst_ref=rcv_i.at[group, mine],
@@ -437,12 +454,15 @@
 
         def increments(p):
             loc = loc_buf[p]
-            a = rcv_e[p, :slots].astype(F32) * jnp.where(at_slot < items, loc, pltpu.roll(loc, items, 0))
-            b = rcv_e[p, slots : 2 * slots].astype(F32) * jnp.where(at_slot < items, loc, pltpu.roll(loc, items - spare, 0))
+            a = ens_rows(p, 0, slots) * jnp.where(at_slot < items, loc, pltpu.roll(loc, items, 0))
+            b = ens_rows(p, slots, 2 * slots) * jnp.where(at_slot < items, loc, pltpu.roll(loc, items - spare, 0))
             rest = total_slots - 2 * slots
-            c = rcv_e[p, 2 * slots :].astype(F32) * loc[2 * spare : 2 * spare + rest]
+            c = ens_rows(p, 2 * slots, total_slots) * loc[2 * spare : 2 * spare + rest]
             hi, lo = split2(jnp.concatenate([a, b, c], axis=0))
             return spread * dot(pick[...], jnp.concatenate([hi, lo], axis=0))
+
+        def offset(i):
+            return (i + low) % parts
 
         def put_increments(i):
             after, before = tiles[i - 1][:, :LANES], tiles[(i + 1) % parts][:, cols - LANES :]
@@ -454,16 +474,16 @@
                 if 3 * per - per * v:
                     moved = pltpu.roll(moved, 3 * per - per * v, 0)
                 pieces[0] = jnp.where(window, moved, pieces[0])
-            snd_i[i] = jnp.concatenate(pieces, axis=0).astype(BF16)
+            snd_i[offset(i)] = jnp.concatenate(pieces, axis=0).astype(BF16)
 
         batch = owners // BATCHES
         for first_of in range(0, owners, batch):
             blocks = [i for k in range(first_of, first_of + batch) for i in (k, k + owners)]
             for i in blocks:
-                if i > 0:
-                    enses.receive(i)
+                if offset(i) > 0:
+                    enses.receive(offset(i))
             for i in blocks:
-                tiles[i] = increments(lax.rem(part + parts - i, parts))
+                tiles[i] = increments(lax.rem(part + parts - offset(i), parts))
             ready = [i for k in range(first_of - 1, first_of + batch - 1) if k > 0 for i in (k, k + owners)]
             if first_of + batch == owners:
                 ready += [owners - 1, parts - 1, 0, owners]
@@ -471,8 +491,8 @@
                 put_increments(i)
             for i in ready:
                 for j in range(groups):
-                    if i + j > 0:
-                        inc_copy(i, j).start()
+                    if offset(i) + j > 0:
+                        inc_copy(offset(i), j).start()
         rcv_i[group, mine] = snd_i[0]
 
     for copy in field_copies:
@@ -554,12 +574,12 @@
                 return out
 
             third = field_of(2, items)
-            a = rcv_e[p, :slots].astype(F32) * jnp.where(at_slot < items, field_of(0, items), pltpu.roll(third, items, 0))
-            b = rcv_e[p, slots : 2 * slots].astype(F32) * jnp.where(
+            a = ens_rows(p, 0, slots) * jnp.where(at_slot < items, field_of(0, items), pltpu.roll(third, items, 0))
+            b = ens_rows(p, slots, 2 * slots) * jnp.where(
                 at_slot < items, field_of(1, items), pltpu.roll(third, items - spare, 0)
             )
             rest = total_slots - 2 * slots
-            c = rcv_e[p, 2 * slots :].astype(F32) * third[2 * spare : 2 * spare + rest]
+            c = ens_rows(p, 2 * slots, total_slots) * third[2 * spare : 2 * spare + rest]
             own = jnp.concatenate([jnp.zeros((2 * spare, cols), F32), c], axis=0)[:slots]
             own = jnp.where(at_slot < 2 * spare, pltpu.roll(b, slots - (items - spare), 0), own)
             own = jnp.where(at_slot < spare, pltpu.roll(a, slots - items, 0), own)
@@ -650,6 +670,7 @@
         *tables(parts, cols, loc_spectrum.shape[0], members, rows),
     )
     packed = (round8(halves * items), LANES)
+    ens_packed = (round8(3 * halves * items), LANES)
     message = (8 * halves, LANES)
     vmem = pl.BlockSpec(memory_space=pltpu.VMEM)
     dma = pltpu.SemaphoreType.DMA
@@ -665,7 +686,7 @@
             *[pltpu.VMEM(t.shape, t.dtype) for t in operands],
             pltpu.VMEM((owners, *packed), F32),
             pltpu.VMEM((parts, *packed), F32),
-            pltpu.VMEM((owners, total_slots, cols), F32),
+            pltpu.VMEM((owners, *ens_packed), F32),
             pltpu.VMEM((parts, slots, cols), F32),
             pltpu.VMEM((3, rows, cols), F32),
             pltpu.VMEM((round8(residues), 4 * inner), F32),
@@ -673,7 +694,7 @@
             pltpu.VMEM((9, rows, cols + LANES), F32),
             pltpu.VMEM((owners, *message), F32),
             pltpu.VMEM((owners, *packed), BF16), pltpu.VMEM((parts, *packed), BF16),
-            pltpu.VMEM((owners, total_slots, cols), BF16), pltpu.VMEM((parts, total_slots, cols), BF16),
+            pltpu.VMEM((owners, *ens_packed), BF16), pltpu.VMEM((parts, *ens_packed), BF16),
             pltpu.VMEM((parts, *message), BF16), pltpu.VMEM((groups, owners, *message), BF16),
             pltpu.VMEM((owners, *message), BF16), pltpu.VMEM((parts, *message), BF16),
             pltpu.VMEM((parts, *packed), BF16), pltpu.VMEM((owners, *packed), BF16),

time: 32.2 us -> 31.6 us (0.981)
  Pallas kernels: 31.4 us -> 30.8 us
    pallas_call x1, Pallas kernels: 30.7 us -> 30.1 us  [per_device(): pl.pallas_call(functools.partial(kernel, groups, parts, spread), out_shap...]
where the time goes in v6:
time: 31.6 us; the launch traced here: 31.5 us
  Pallas kernels  30.8 us (97%)
  between operations  0.64 us (2%)
    pallas_call x1, Pallas kernels, per_device(): pl.pallas_call(functools.partial(kernel, groups, parts, spread), out_shap...  30.1 us
    pallas_call x1, Pallas kernels, per_device(): pl.pallas_call(finish, out_shape=(jax.ShapeDtypeStruct(alpha.shape, F32),...  0.69 us

profile of v6, /device:TPU:0, one launch (start us, length us, event | category | flops | bytes accessed | tf_op | source)
XLA Modules:
  0.0 31.5 jit_solution(326494758698778313)
XLA Ops:
  0.6 30.1 %shard_map.167 = (f32[10,16,256]{2,1,0:T(8,128)S(1)}, f32[3,8,256]{2,1,0:T(8,128)S(1)}) custom-call(f32[10,16,256]{2,1,0:T(8,128)} %alpha_any.1, bf16[10,3,16,256]{3,2,1,0:T(8,128)(2,1)} %ens_any.1, f32[3,8,256]{2,1,0:T(8,128)} %std_any.1, f32[3,8,256]{2,1,0:T(8,128)} %control_any.1, f32[1,1024]{1,0:T(1,128)} %bitcast.5, s32[1,1024]{1,0:T(1,128)} %bitcast.6, ...), custom_call_target="tpu_custom_call" | custom-call | tf_op jit(solution)/shard_map/pallas_call | solution.py:677
  30.8 0.7 %shard_map.168 = (f32[10,16,256]{2,1,0:T(8,128)}, f32[3,8,256]{2,1,0:T(8,128)}) custom-call(f32[10,16,256]{2,1,0:T(8,128)S(1)} %get-tuple-element.4.corr_ref, f32[3,8,256]{2,1,0:T(8,128)S(1)} %get-tuple-element.5.grad_control_ref), custom_call_target="tpu_custom_call" | custom-call | tf_op jit(solution)/shard_map/pallas_call | solution.py:712

commit v7 on v6

--- a/solution.py
+++ b/solution.py
@@ -242,6 +242,16 @@
                 src_ref=self.source.at[0], dst_ref=self.target.at[at],
                 send_sem=self.send.at[0], recv_sem=self.recv.at[at], device_id={"sp": left},
             ).wait_recv()
+
+        def receive_from(self, p):
+            arrival = pltpu.make_async_remote_copy(
+                src_ref=self.source.at[0], dst_ref=self.target.at[p],
+                send_sem=self.send.at[0], recv_sem=self.recv.at[p], device_id={"sp": left},
+            )
+            if low <= p < low + owners:
+                pl.when(part != p)(arrival.wait_recv)
+            else:
+                arrival.wait_recv()
 
         def finish(self):
             for i in range(owners):
@@ -509,6 +519,8 @@
             else:
                 wide[f, at, cols:] = jnp.zeros((tile_rows, LANES), F32)
 
+    row_at = lax.broadcasted_iota(jnp.int32, (rows, cols + LANES), 0).astype(F32)
+    rotation = 0.1 + 0.2 * (row_at + 0.5) / rows
     for j in range(groups):
         for k in range(owners):
             g, at = lax.rem(group + j, groups), lax.rem(part + k, owners)
@@ -534,13 +546,10 @@
         pieces = [gathered(8 * h + per * v) for h in range(halves)]
         pieces.append(pltpu.roll(ends, LANES - (2 * HALO * v + HALO), 1))
         state0.append(jnp.concatenate(pieces, axis=1) + wide[v])
-    row_at = lax.broadcasted_iota(jnp.int32, (rows, cols + LANES), 0).astype(F32)
-    rotation = 0.1 + 0.2 * (row_at + 0.5) / rows
     state1 = model_step(state0, rotation)
     state2 = model_step(state1, rotation)
     forcing = [wide[3 + t] * s[0] - wide[6 + t] for t, s in enumerate((state0, state1, state2))]
-    zero = jnp.zeros_like(rotation)
-    h, u, w = adjoint_step((forcing[2], zero, zero), rotation)
+    h, u, w = forcing[2], COURANT * dx(forcing[2]), COURANT * dy(forcing[2])
     h, u, w = adjoint_step((h + forcing[1], u, w), rotation)
     for v, field in enumerate((h + forcing[0], u, w)):
         field = field[:, :cols]
@@ -557,10 +566,15 @@
     @pl.when(owner)
     def _():
         halfs.take_own()
-        for i in range(1, parts):
-            halfs.receive(i)
-        weighted = []
-        for p in range(parts):
+        weighted = [None] * parts
+        middle = range(low, low + owners)
+        for p in middle:
+            halfs.receive_from(p)
+        for p in [*middle, *[p for p in range(parts) if p not in middle]]:
+            if p == 0:
+                for other in range(parts):
+                    if other not in middle:
+                        halfs.receive_from(other)
             came_h = rcv_h[p].astype(F32)
 
             def row_of(v, j):
@@ -583,7 +597,7 @@
             own = jnp.concatenate([jnp.zeros((2 * spare, cols), F32), c], axis=0)[:slots]
             own = jnp.where(at_slot < 2 * spare, pltpu.roll(b, slots - (items - spare), 0), own)
             own = jnp.where(at_slot < spare, pltpu.roll(a, slots - items, 0), own)
-            weighted.append(a + b + own)
+            weighted[p] = a + b + own
         outs = filtered([[x[:, h * LANES : (h + 1) * LANES] for x in weighted] for h in range(halves)], False)
         for p in range(parts):
             for h in range(halves):
@@ -600,7 +614,7 @@
             send_sem=o_send.at[0], recv_sem=o_recv.at[at], device_id={"sp": left},
         )
         pl.when(at != mine)(arrival.wait_recv)
-    stage[...] = rcv_o[...].astype(F32)
+        stage[at] = rcv_o[at].astype(F32)
     for m in range(members):
         for j in range(per):
             for h in range(halves):

time: 31.6 us -> 31.5 us (level)
  no operation moved by 1% of the time
where the time goes in v7:
time: 31.5 us; the launch traced here: 31.4 us
  Pallas kernels  30.7 us (97%)
  between operations  0.64 us (2%)
    pallas_call x1, Pallas kernels, per_device(): pl.pallas_call(functools.partial(kernel, groups, parts, spread), out_shap...  30 us
    pallas_call x1, Pallas kernels, per_device(): pl.pallas_call(finish, out_shape=(jax.ShapeDtypeStruct(alpha.shape, F32),...  0.69 us

profile of v7, /device:TPU:0, one launch (start us, length us, event | category | flops | bytes accessed | tf_op | source)
XLA Modules:
  0.0 31.4 jit_solution(4864208483961690745)
XLA Ops:
  0.6 30.0 %shard_map.167 = (f32[10,16,256]{2,1,0:T(8,128)S(1)}, f32[3,8,256]{2,1,0:T(8,128)S(1)}) custom-call(f32[10,16,256]{2,1,0:T(8,128)} %alpha_any.1, bf16[10,3,16,256]{3,2,1,0:T(8,128)(2,1)} %ens_any.1, f32[3,8,256]{2,1,0:T(8,128)} %std_any.1, f32[3,8,256]{2,1,0:T(8,128)} %control_any.1, f32[1,1024]{1,0:T(1,128)} %bitcast.5, s32[1,1024]{1,0:T(1,128)} %bitcast.6, ...), custom_call_target="tpu_custom_call" | custom-call | tf_op jit(solution)/shard_map/pallas_call | solution.py:691
  30.7 0.7 %shard_map.168 = (f32[10,16,256]{2,1,0:T(8,128)}, f32[3,8,256]{2,1,0:T(8,128)}) custom-call(f32[10,16,256]{2,1,0:T(8,128)S(1)} %get-tuple-element.4.corr_ref, f32[3,8,256]{2,1,0:T(8,128)S(1)} %get-tuple-element.5.grad_control_ref), custom_call_target="tpu_custom_call" | custom-call | tf_op jit(solution)/shard_map/pallas_call | solution.py:726

commit v8 on v7

--- a/solution.py
+++ b/solution.py
@@ -207,61 +207,6 @@
                 )
     snd_a[...] = stage[...].astype(BF16)
 
-    @pl.when(owner)
-    def _():
-        pl.semaphore_wait(barrier, owners + groups - 2)
-
-    @pl.when(jnp.logical_not(owner))
-    def _():
-        pl.semaphore_wait(barrier, owners + groups - 1)
-        for i in range(owners):
-            pl.semaphore_signal(here, inc=1, device_id={"sp": low + lax.rem(part + i, owners)})
-
-    class ToOwners:
-        def __init__(self, source, target, send, recv):
-            self.source, self.target, self.send, self.recv = source, target, send, recv
-
-        def copy(self, i):
-            at = lax.rem(part + i, owners)
-            return low + at, pltpu.make_async_remote_copy(
-                src_ref=self.source.at[at], dst_ref=self.target.at[part],
-                send_sem=self.send.at[i], recv_sem=self.recv.at[part], device_id={"sp": low + at},
-            )
-
-        def start(self):
-            for i in range(owners):
-                to, copy = self.copy(i)
-                pl.when(to != part)(copy.start)
-
-        def take_own(self):
-            self.target[part] = self.source[mine]
-
-        def receive(self, i):
-            at = lax.rem(part + parts - i, parts)
-            pltpu.make_async_remote_copy(
-                src_ref=self.source.at[0], dst_ref=self.target.at[at],
-                send_sem=self.send.at[0], recv_sem=self.recv.at[at], device_id={"sp": left},
-            ).wait_recv()
-
-        def receive_from(self, p):
-            arrival = pltpu.make_async_remote_copy(
-                src_ref=self.source.at[0], dst_ref=self.target.at[p],
-                send_sem=self.send.at[0], recv_sem=self.recv.at[p], device_id={"sp": left},
-            )
-            if low <= p < low + owners:
-                pl.when(part != p)(arrival.wait_recv)
-            else:
-                arrival.wait_recv()
-
-        def finish(self):
-            for i in range(owners):
-                to, copy = self.copy(i)
-                pl.when(to != part)(copy.wait_send)
-
-    alphas = ToOwners(snd_a, rcv_a, a_send, a_recv)
-    enses = ToOwners(snd_e, rcv_e, e_send, e_recv)
-    halfs = ToOwners(snd_h, rcv_h, h_send, h_recv)
-    alphas.start()
     loads[1].wait()
     if ens_stage.shape[1] > halves * used:
         ens_stage[:, halves * used :, :] = jnp.zeros((owners, ens_stage.shape[1] - halves * used, LANES), F32)
@@ -273,6 +218,61 @@
                     at = half_row(slot_of(v, j * members + m, items, slots, spare), h, halves, used)
                     ens_stage[:, at, :] = field[j * owners : (j + 1) * owners, h * LANES : (h + 1) * LANES]
     snd_e[...] = ens_stage[...].astype(BF16)
+    @pl.when(owner)
+    def _():
+        pl.semaphore_wait(barrier, owners + groups - 2)
+
+    @pl.when(jnp.logical_not(owner))
+    def _():
+        pl.semaphore_wait(barrier, owners + groups - 1)
+        for i in range(owners):
+            pl.semaphore_signal(here, inc=1, device_id={"sp": low + lax.rem(part + i, owners)})
+
+    class ToOwners:
+        def __init__(self, source, target, send, recv):
+            self.source, self.target, self.send, self.recv = source, target, send, recv
+
+        def copy(self, i):
+            at = lax.rem(part + i, owners)
+            return low + at, pltpu.make_async_remote_copy(
+                src_ref=self.source.at[at], dst_ref=self.target.at[part],
+                send_sem=self.send.at[i], recv_sem=self.recv.at[part], device_id={"sp": low + at},
+            )
+
+        def start(self):
+            for i in range(owners):
+                to, copy = self.copy(i)
+                pl.when(to != part)(copy.start)
+
+        def take_own(self):
+            self.target[part] = self.source[mine]
+
+        def receive(self, i):
+            at = lax.rem(part + parts - i, parts)
+            pltpu.make_async_remote_copy(
+                src_ref=self.source.at[0], dst_ref=self.target.at[at],
+                send_sem=self.send.at[0], recv_sem=self.recv.at[at], device_id={"sp": left},
+            ).wait_recv()
+
+        def receive_from(self, p):
+            arrival = pltpu.make_async_remote_copy(
+                src_ref=self.source.at[0], dst_ref=self.target.at[p],
+                send_sem=self.send.at[0], recv_sem=self.recv.at[p], device_id={"sp": left},
+            )
+            if low <= p < low + owners:
+                pl.when(part != p)(arrival.wait_recv)
+            else:
+                arrival.wait_recv()
+
+        def finish(self):
+            for i in range(owners):
+                to, copy = self.copy(i)
+                pl.when(to != part)(copy.wait_send)
+
+    alphas = ToOwners(snd_a, rcv_a, a_send, a_recv)
+    enses = ToOwners(snd_e, rcv_e, e_send, e_recv)
+    halfs = ToOwners(snd_h, rcv_h, h_send, h_recv)
+    alphas.start()
     enses.start()
 
     for load in loads[2:8]:

time: 31.5 us -> 31.5 us (level)
  no operation moved by 1% of the time
where the time goes in v8:
time: 31.5 us; the launch traced here: 31.4 us
  Pallas kernels  30.7 us (97%)
  between operations  0.64 us (2%)
    pallas_call x1, Pallas kernels, per_device(): pl.pallas_call(functools.partial(kernel, groups, parts, spread), out_shap...  30 us
    pallas_call x1, Pallas kernels, per_device(): pl.pallas_call(finish, out_shape=(jax.ShapeDtypeStruct(alpha.shape, F32),...  0.69 us

profile of v8, /device:TPU:0, one launch (start us, length us, event | category | flops | bytes accessed | tf_op | source)
XLA Modules:
  0.0 31.4 jit_solution(2758699953881543915)
XLA Ops:
  0.6 30.0 %shard_map.167 = (f32[10,16,256]{2,1,0:T(8,128)S(1)}, f32[3,8,256]{2,1,0:T(8,128)S(1)}) custom-call(f32[10,16,256]{2,1,0:T(8,128)} %alpha_any.1, bf16[10,3,16,256]{3,2,1,0:T(8,128)(2,1)} %ens_any.1, f32[3,8,256]{2,1,0:T(8,128)} %std_any.1, f32[3,8,256]{2,1,0:T(8,128)} %control_any.1, f32[1,1024]{1,0:T(1,128)} %bitcast.5, s32[1,1024]{1,0:T(1,128)} %bitcast.6, ...), custom_call_target="tpu_custom_call" | custom-call | tf_op jit(solution)/shard_map/pallas_call | solution.py:691
  30.7 0.7 %shard_map.168 = (f32[10,16,256]{2,1,0:T(8,128)}, f32[3,8,256]{2,1,0:T(8,128)}) custom-call(f32[10,16,256]{2,1,0:T(8,128)S(1)} %get-tuple-element.4.corr_ref, f32[3,8,256]{2,1,0:T(8,128)S(1)} %get-tuple-element.5.grad_control_ref), custom_call_target="tpu_custom_call" | custom-call | tf_op jit(solution)/shard_map/pallas_call | solution.py:726

commit v9 on v7

--- a/solution.py
+++ b/solution.py
@@ -468,8 +468,7 @@
             b = ens_rows(p, slots, 2 * slots) * jnp.where(at_slot < items, loc, pltpu.roll(loc, items - spare, 0))
             rest = total_slots - 2 * slots
             c = ens_rows(p, 2 * slots, total_slots) * loc[2 * spare : 2 * spare + rest]
-            hi, lo = split2(jnp.concatenate([a, b, c], axis=0))
-            return spread * dot(pick[...], jnp.concatenate([hi, lo], axis=0))
+            return spread * dot(pick[:, :total_slots], jnp.concatenate([a, b, c], axis=0).astype(BF16))
 
         def offset(i):
             return (i + low) % parts

time: 31.5 us -> 31.5 us (level)
  no operation moved by 1% of the time
where the time goes in v9:
time: 31.5 us; the launch traced here: 31.3 us
  Pallas kernels  30.7 us (97%)
  between operations  0.64 us (2%)
    pallas_call x1, Pallas kernels, per_device(): pl.pallas_call(functools.partial(kernel, groups, parts, spread), out_shap...  30 us
    pallas_call x1, Pallas kernels, per_device(): pl.pallas_call(finish, out_shape=(jax.ShapeDtypeStruct(alpha.shape, F32),...  0.69 us

profile of v9, /device:TPU:0, one launch (start us, length us, event | category | flops | bytes accessed | tf_op | source)
XLA Modules:
  0.0 31.3 jit_solution(15127467686145378513)
XLA Ops:
  0.6 30.0 %shard_map.167 = (f32[10,16,256]{2,1,0:T(8,128)S(1)}, f32[3,8,256]{2,1,0:T(8,128)S(1)}) custom-call(f32[10,16,256]{2,1,0:T(8,128)} %alpha_any.1, bf16[10,3,16,256]{3,2,1,0:T(8,128)(2,1)} %ens_any.1, f32[3,8,256]{2,1,0:T(8,128)} %std_any.1, f32[3,8,256]{2,1,0:T(8,128)} %control_any.1, f32[1,1024]{1,0:T(1,128)} %bitcast.5, s32[1,1024]{1,0:T(1,128)} %bitcast.6, ...), custom_call_target="tpu_custom_call" | custom-call | tf_op jit(solution)/shard_map/pallas_call | solution.py:690
  30.7 0.7 %shard_map.168 = (f32[10,16,256]{2,1,0:T(8,128)}, f32[3,8,256]{2,1,0:T(8,128)}) custom-call(f32[10,16,256]{2,1,0:T(8,128)S(1)} %get-tuple-element.4.corr_ref, f32[3,8,256]{2,1,0:T(8,128)S(1)} %get-tuple-element.5.grad_control_ref), custom_call_target="tpu_custom_call" | custom-call | tf_op jit(solution)/shard_map/pallas_call | solution.py:725
